TPU v7x, 512 devices: a whole 4x4x16 slice. The times are simulated.
512 devices in a mesh: zero: 8 (over x, core), cols: 64 (over z, y).
Axes of the slice: x: 4, y: 4, z: 16, core: 2. Of those that a mesh axis runs over, the one named last changes fastest.
Arguments:
- train_gate: bfloat16 [5120, 25600], P('zero', 'cols'), may hold values from -0.25 to 0.25
- low_gate: bfloat16 [5120, 64], P('zero'), may hold values from -0.078125 to 0.078125
- high_gate: bfloat16 [64, 25600], P(None, 'cols'), may hold values from -0.75 to 0.75
- train_up: bfloat16 [5120, 25600], P('zero', 'cols'), may hold values from -0.25 to 0.25
- low_up: bfloat16 [5120, 64], P('zero'), may hold values from -0.078125 to 0.078125
- high_up: bfloat16 [64, 25600], P(None, 'cols'), may hold values from -0.75 to 0.75
- norm_train: float32 [5120], P(('zero', 'cols')), may hold values from 0.25 to 1.75
- norm_step: float32 [5120], P(('zero', 'cols')), may hold values from -0.3 to 0.3
Outputs:
- ready_gate: bfloat16 [5120, 25600], P(None, 'cols')
- ready_up: bfloat16 [5120, 25600], P(None, 'cols')
- column_gate: float32 [25600], P('cols')
- column_up: float32 [25600], P('cols')
- serve_norm: bfloat16 [5120], replicated
All inputs are finite; a program needn't handle non-finite values.
Results may differ from a plain program's by a relative error of at most 0.001.
Values may be sent and summed in bfloat16 or wider, within the bound.
A program may use at most 128 MiB of HBM per device.

v0:
```python
import jax
import jax.numpy as jnp
from jax import lax
from jax.sharding import Mesh
from jax.sharding import PartitionSpec as P

ZERO = ("zero_0", "zero_1")
ZERO_COLS = ("zero_0", "zero_1", "cols_0", "cols_1")
COLS = ("cols_0", "cols_1")


mix_rate = 2.0


def from_everyone(x, axis):
    copies = jnp.broadcast_to(x, (lax.axis_size(axis), *x.shape))
    return lax.all_to_all(copies, axis, split_axis=0, concat_axis=0, tiled=True)


def over_copies(x, axis):
    everything = from_everyone(x, axis)
    return jnp.sum(everything, axis=0)


def in_one(arrays, axis):
    flat, at, outs = (jnp.concatenate([a.reshape(-1) for a in arrays]), 0, [])
    subtotal = over_copies(flat, axis)
    for a in arrays:
        outs.append(subtotal[at : at + a.size].reshape(a.shape))
        at += a.size
    return tuple(outs)


def in_one_piece(arrays, axis, dim, along):
    widths = [a.shape[along] for a in arrays]
    both = jnp.concatenate(arrays, axis=along)
    result = lax.all_gather(both, axis, axis=dim, tiled=True)
    return tuple(jnp.split(result, [sum(widths[:k]) for k in range(1, len(widths))], axis=along))


def laid_out(parts, dim):
    parts = jnp.moveaxis(parts, 0, dim)
    shape = parts.shape
    return parts.reshape(*shape[:dim], shape[dim] * shape[dim + 1], *shape[dim + 2 :])


def stacked_from(x, axes, turns):
    parts = x[None]
    for k in turns:
        parts = lax.all_gather(parts, axes[k], axis=0, tiled=True)
    block = [lax.axis_size(axes[k]) for k in reversed(turns)]
    parts = parts.reshape(*block, *x.shape)
    turned = sorted(range(len(turns)), key=lambda place: turns[len(turns) - 1 - place])
    return parts.transpose(*turned, *range(len(turns), parts.ndim)).reshape(-1, *x.shape)


def gather_axes(x, axes, turns, dim):
    return laid_out(stacked_from(x, axes, turns), dim)


def on_device(train_gate, low_gate, high_gate, train_up, low_up, high_up, norm_train, norm_step):
    latest_gate = train_gate.astype(jnp.float32) + mix_rate * jnp.dot(
        low_gate, high_gate, preferred_element_type=jnp.float32
    )
    latest_up = train_up.astype(jnp.float32) + mix_rate * jnp.dot(
        low_up, high_up, preferred_element_type=jnp.float32
    )
    total_gate, total_up = in_one(
        (jnp.sum(latest_gate * latest_gate, axis=0), jnp.sum(latest_up * latest_up, axis=0)), ZERO
    )
    column_gate = jnp.sqrt(total_gate)
    column_up = jnp.sqrt(total_up)
    narrow_gate, narrow_up = (
        (latest_gate / column_gate).astype(jnp.bfloat16),
        (latest_up / column_up).astype(jnp.bfloat16),
    )
    ready_gate, ready_up = in_one_piece((narrow_gate, narrow_up), ZERO, 0, 1)
    serve_norm = gather_axes(
        (norm_train + norm_step).astype(jnp.bfloat16), ZERO_COLS, (0, 3, 2, 1), 0
    )
    return (ready_gate, ready_up, column_gate, column_up, serve_norm)


def solution(mesh):
    finer = Mesh(mesh.devices.reshape(4, 2, 16, 4), ("zero_0", "zero_1", "cols_0", "cols_1"))
    return jax.shard_map(
        on_device,
        mesh=finer,
        in_specs=(
            P(ZERO, COLS),
            P(ZERO, None),
            P(None, COLS),
            P(ZERO, COLS),
            P(ZERO, None),
            P(None, COLS),
            P(ZERO_COLS),
            P(ZERO_COLS),
        ),
        out_specs=(P(None, COLS), P(None, COLS), P(COLS), P(COLS), P()),
        check_vma=False,
    )
```

profile of v0, /device:TPU:1, one launch (start us, length us, event | category | flops | bytes accessed | tf_op | source)
XLA Modules:
  0.0 95.7 jit_solution(9329945814760136430)
XLA Ops:
  7.2 0.0 copy-start
  7.2 0.0 all-gather.4.cloned.1.call-start
  7.2 0.8 copy-done
  8.1 1.6 %multiply_reduce_fusion.1 = (f32[400]{0:T(512)S(1)}, f32[640,400]{0,1:T(8,128)S(1)}) fusion(bf16[640,64]{0,1:T(8,128)(2,1)S(1)} %copy-done, bf16[64,400]{1,0:T(8,128)(2,1)} %param.10, bf16[640,400]{0,1:T(8,128)(2,1)} %param.8), kind=kOutput, calls=%fused_computation.8 | convolution fusion | flops 34047600 | bytes 1670720 | tf_op jit(solution)/shard_map/dot_general | solution.py:62
  9.6 0.0 copy-start.3
  9.6 0.0 copy-start.4
  9.6 1.6 %multiply_reduce_fusion = (f32[400]{0:T(512)S(1)}, f32[640,400]{0,1:T(8,128)S(1)}) fusion(bf16[640,64]{0,1:T(8,128)(2,1)} %param.12, bf16[64,400]{1,0:T(8,128)(2,1)} %param.13, bf16[640,400]{0,1:T(8,128)(2,1)} %param.11), kind=kOutput, calls=%fused_computation.7 | convolution fusion | flops 34047600 | bytes 1670720 | tf_op jit(solution)/shard_map/dot_general | solution.py:65
  11.3 0.1 pad_maximum_fusion.1
  11.4 13.9 %all_to_all.6 = f32[8,1,800]{2,1,0:T(1,128)S(1)} all-to-all(f32[8,1,800]{2,1,0:T(1,128)S(1)} %broadcast_in_dim.8), channel_id=1, replica_groups=mesh['zero_0'=4,'zero_1'=2,'cols_0'=16,'cols_1'=4] {'zero_0','zero_1'}, dimensions={0} | all-to-all | bytes 51200 | tf_op jit(solution)/shard_map/all_to_all | solution.py:17
  25.3 0.1 slice_sqrt_fusion.1
  25.4 0.0 copy-start.1
  25.4 0.0 copy-start.2
  25.4 0.2 divide_convert_fusion
  25.6 1.0 %pad_maximum_fusion = bf16[640,800]{0,1:T(8,128)(2,1)} fusion(bf16[640,400]{0,1:T(8,128)(2,1)S(1)} %get-tuple-element.13, bf16[640,400]{0,1:T(8,128)(2,1)S(1)} %get-tuple-element.14), kind=kLoop, calls=%fused_computation.4 | loop fusion | flops 2048000 | bytes 2048000 | tf_op jit(solution)/shard_map/concatenate | solution.py:36
  26.6 0.0 all-gather.4.cloned.1.call-update
  26.7 1.3 %dynamic-slice = u32[1]{0:T(128)} dynamic-slice(u32[512]{0:T(512)} %constant.12, u32[]{:T(128)S(6)} %add.12), dynamic_slice_sizes={1} | dynamic-slice | bytes 12
  28.6 0.0 copy-done.3
  28.6 0.0 copy-done.4
  28.6 0.2 dynamic-update-slice
  28.9 6.8 %all-reduce = bf16[40]{0:T(256)(128)(2,1)S(1)} all-reduce(bf16[40]{0:T(256)(128)(2,1)S(1)} %dynamic-update-slice), channel_id=2, replica_groups=mesh['zero_0'=4,'zero_1'=2,'cols_0'=16,'cols_1'=4] {'zero_0'}, use_global_device_ids=true, to_apply=%add | all-reduce | flops 40 | bytes 160
  35.7 0.1 reshape.24
  35.8 5.2 %all-gather.1 = bf16[4,4,10]{2,1,0:T(4,128)(2,1)S(1)} all-gather(bf16[1,4,10]{2,1,0:T(4,128)(2,1)S(1)} %reshape.24), channel_id=1, replica_groups=mesh['zero_0'=4,'zero_1'=2,'cols_0'=16,'cols_1'=4] {'cols_1'}, dimensions={0}, use_global_device_ids=true | all-gather | bytes 400 | tf_op jit(solution)/shard_map/all_gather | solution.py:50
  41.1 30.8 %all_gather.18 = bf16[256,10]{1,0:T(8,128)(2,1)S(1)} all-gather(bf16[16,10]{1,0:T(8,128)(2,1)S(1)} %bitcast.10), channel_id=1, replica_groups=mesh['zero_0'=4,'zero_1'=2,'cols_0'=16,'cols_1'=4] {'cols_0'}, dimensions={0}, use_global_device_ids=true | all-gather | bytes 5440 | tf_op jit(solution)/shard_map/all_gather | solution.py:50
  71.9 10.3 %all_gather.19 = bf16[512,10]{1,0:T(8,128)(2,1)S(1)} all-gather(bf16[256,10]{1,0:T(8,128)(2,1)S(1)} %all_gather.18), channel_id=1, replica_groups=mesh['zero_0'=4,'zero_1'=2,'cols_0'=16,'cols_1'=4] {'zero_1'}, dimensions={0}, use_global_device_ids=true | all-gather | bytes 15360 | tf_op jit(solution)/shard_map/all_gather | solution.py:50
  82.2 0.1 copy.17
  82.3 0.8 reshape_reshape.3
  83.1 0.0 all-gather.4.cloned.1.call-done
  83.1 5.8 %fusion.2 = (bf16[5120,400]{0,1:T(8,128)(2,1)}, bf16[5120,400]{0,1:T(8,128)(2,1)}) fusion(bf16[5120,800]{0,1:T(8,128)(2,1)} %all-gather.4.cloned.1.call-done), kind=kLoop, calls=%fused_computation.13 | loop fusion | bytes 16384000 | tf_op jit(solution)/shard_map/split | solution.py:38
  88.8 0.0 copy-done.1
  88.8 0.0 copy-done.2
  (4 shorter events, 0.1 us)
Async XLA Ops:
  7.2 0.9 copy-start
  7.2 75.9 %all-gather.4.cloned.1.call-start = ((), (), s32[]{:S(2)}) async-start(), calls=%async_computation.1 | async-start | bytes 9216000 | tf_op jit(solution)/shard_map/all_gather | solution.py:37
  9.6 19.0 %copy-start.3 = (f32[10]{0:T(128)S(1)}, f32[10]{0:T(128)}, u32[]{:S(2)}) copy-start(f32[10]{0:T(128)} %param.14) | copy-start | bytes 124
  9.6 19.0 %copy-start.4 = (f32[10]{0:T(128)S(1)}, f32[10]{0:T(128)}, u32[]{:S(2)}) copy-start(f32[10]{0:T(128)} %param.15) | copy-start | bytes 124
  25.4 63.5 %copy-start.1 = (f32[400]{0:T(512)}, f32[400]{0:T(512)S(1)}, u32[]{:S(2)}) copy-start(f32[400]{0:T(512)S(1)} %get-tuple-element.7) | copy-start | bytes 4804
  25.4 63.5 %copy-start.2 = (f32[400]{0:T(512)}, f32[400]{0:T(512)S(1)}, u32[]{:S(2)}) copy-start(f32[400]{0:T(512)S(1)} %get-tuple-element.8) | copy-start | bytes 4804
Sparse Core Ops, SparseCore 0:
  26.8 55.8 all-gather.3
where the time goes:
time: 96 us; the launch traced here: 95.7 us
  blocking collectives  67.1 us (70%)
  between operations  14.8 us (15%)
  local copies, waits for them, and re-layouts  9.18 us (10%)
  matrix products  3.18 us (3%)
  other arithmetic  1.38 us (1%)
    all_gather x3, blocking collectives, stacked_from(): parts = lax.all_gather(parts, axes[k], axis=0, tiled=True)  46.4 us
    all_to_all x1, blocking collectives, from_everyone(): return lax.all_to_all(copies, axis, split_axis=0, concat_axis=0, tiled=True)  13.9 us
    unnamed x1, blocking collectives  6.85 us
    split x1, local copies, waits for them, and re-layouts, in_one_piece(): jnp.split(result, [sum(widths[:k]) for k in range(1, len(widths))], axis=...  5.78 us
    unnamed x14, local copies, waits for them, and re-layouts  2.46 us
  transfers between devices with their start and end apart: 1, of which 0 were waited for; matrix products, arithmetic and copies ran while one was open for 3% of the time, Pallas kernels for 0%

commit v1 on v0

v1 whole, which is shorter than its diff:
```python
import functools

import jax
import jax.numpy as jnp
from jax import lax
from jax.experimental import pallas as pl
from jax.experimental.pallas import tpu as pltpu
from jax.sharding import PartitionSpec as P

F32, BF16 = jnp.float32, jnp.bfloat16
MESH = pl.DeviceIdType.MESH

NX, NC, NY, NZ = 4, 2, 4, 16
GROUP = NX * NC
D_MODEL, WIDE, RANK = 5120, 400, 64
ROWS = D_MODEL // GROUP
LANES = 128
STRIPS = ROWS // LANES
NCH = 2 * STRIPS
PAIRS = NCH // 2
MAIN, TAIL = 384, 16
STEP = 80
OWN, LEFT, RIGHT, FAR = 0, 1, 2, 3
PER = 10
NORM_ROWS = D_MODEL // LANES


def gather_kernel(
    tg, lg, hg, tu, lu, hu, nt, ns,
    out, col, norm,
    tv, lv, hv, ht, ntv, nsv,
    lat, part, spread, sums, ny, zr, zl, nscr,
    load_sem, sum_send, sum_recv,
    p_send, m_send, f_send, l_recv, r_recv, o_recv, d_send, d_recv,
    y_send, y_recv, zr_send, zr_recv, zl_send, zl_recv,
):
    me = lax.axis_index("zero")
    cols = lax.axis_index("cols")
    x, c = me // NC, me % NC
    z, y = cols // NY, cols % NY

    def chip(dx, core):
        return ((x + dx) % NX) * NC + core

    def at_x(dx, core):
        return (chip(dx, core), cols)

    def at_y(dy):
        return (me, z * NY + (y + dy) % NY)

    def at_z(dz):
        return (me, ((z + dz) % NZ) * NY + y)

    partner = at_x(0, 1 - c)
    plus, minus = at_x(1, c), at_x(NX - 1, c)
    group = [partner]
    for dx in range(1, NX):
        group += [at_x(dx, c), at_x(dx, 1 - c)]

    loads = [
        pltpu.make_async_copy(a, b, load_sem.at[i])
        for i, (a, b) in enumerate(
            ((hg, hv.at[0]), (hu, hv.at[1]), (lg, lv.at[0]), (lu, lv.at[1]),
             (tg, tv.at[0]), (tu, tv.at[1]), (nt, ntv), (ns, nsv))
        )
    ]
    for load in loads:
        load.start()

    barrier = pltpu.get_barrier_semaphore()
    peers = group + [at_y(1), at_y(NY - 1), at_z(1), at_z(NZ - 1)]
    for peer in peers:
        pl.semaphore_signal(barrier, inc=1, device_id=peer, device_id_type=MESH)

    for load in loads[:4]:
        load.wait()

    def dot(a, b):
        return jnp.dot(a, b, preferred_element_type=F32)

    for k in range(2):
        ht[k] = (hv[k].astype(F32).T * 2.0).astype(BF16)
    part[WIDE + TAIL:512, :] = jnp.zeros((512 - WIDE - TAIL, LANES), F32)

    for k in range(2):
        loads[4 + k].wait()
        for q in range(WIDE // STEP):
            r = slice(STEP * q, STEP * q + STEP)
            w = tv[k, r, :].astype(F32) + dot(ht[k, r, :], lv[k])
            lat[k, r, :] = w
            w = w * w
            s = w[:, 0:LANES]
            for t in range(1, STRIPS):
                s = s + w[:, LANES * t:LANES * t + LANES]
            if k == 0:
                part[r, :] = s
            elif r.stop <= MAIN:
                part[512 + r.start:512 + r.stop, :] = s
            else:
                part[512 + r.start:512 + MAIN, :] = s[:MAIN - r.start]
                part[WIDE:WIDE + TAIL, :] = s[MAIN - r.start:]
    loads[6].wait()
    loads[7].wait()

    lane = lax.broadcasted_iota(jnp.int32, (1, LANES), 1)
    gains = jnp.zeros((1, LANES), F32)
    for k in range(PER):
        gains = jnp.where(lane == (cols * PER + k) % LANES, ntv[k] + nsv[k], gains)

    mine = pl.multiple_of(me * 8, 8)
    sums[pl.ds(mine, 8), :] = jnp.concatenate(
        [jnp.sum(part[LANES * t:LANES * t + LANES, :].T, axis=0, keepdims=True) for t in range(7)]
        + [gains], axis=0)

    pl.semaphore_wait(barrier, len(peers))

    def sum_copy(k, peer, source):
        return pltpu.make_async_remote_copy(
            src_ref=sums.at[pl.ds(mine, 8), :],
            dst_ref=sums.at[pl.ds(mine, 8), :],
            send_sem=sum_send.at[k], recv_sem=sum_recv.at[source],
            device_id=peer, device_id_type=MESH)

    for k, peer in enumerate(group):
        sum_copy(k, peer, me).start()
    for k, peer in enumerate(group):
        sum_copy(k, peer, peer[0]).wait_recv()

    total = sums[0:8, :]
    for s in range(1, GROUP):
        total = total + sums[8 * s:8 * s + 8, :]
    column = jnp.sqrt(total)
    inverse = jnp.concatenate([1.0 / column, jnp.zeros((LANES - 8, LANES), F32)], axis=0).T

    def spread_out(k):
        for t in range(3):
            spread[k, LANES * t:LANES * t + LANES, :] = jnp.broadcast_to(
                inverse[:, 4 * k + t:4 * k + t + 1], (LANES, LANES))
        spread[k, MAIN:, :] = jnp.broadcast_to(
            inverse[TAIL * k:TAIL * k + TAIL, 3:4], (TAIL, LANES))

    def block(shard, j):
        return out.at[j // STRIPS, :, pl.ds(
            pl.multiple_of(shard * ROWS + (j % STRIPS) * LANES, LANES), LANES)]

    def remote(ref, send, recv, dev):
        return pltpu.make_async_remote_copy(
            src_ref=ref, dst_ref=ref, send_sem=send, recv_sem=recv,
            device_id=dev, device_id_type=MESH)

    source = [me, chip(NX - 1, c), chip(1, c), chip(2, c)]
    twin = [chip(0, 1 - c), chip(NX - 1, 1 - c), chip(1, 1 - c), chip(2, 1 - c)]

    def by_plus(j, shard=me):
        return remote(block(shard, j), p_send.at[j], l_recv.at[j], plus)

    def by_minus(j, shard=me):
        return remote(block(shard, j), m_send.at[j], r_recv.at[j], minus)

    def onward_plus(j, shard=source[LEFT]):
        return remote(block(shard, j), f_send.at[j], o_recv.at[j], plus)

    def onward_minus(j):
        return remote(block(source[RIGHT], j), f_send.at[j], o_recv.at[j], minus)

    def across(k, j, shards=source):
        return remote(block(shards[k], j), d_send.at[k * NCH + j], d_recv.at[k * NCH + j], partner)

    def make(k, t):
        j = k * STRIPS + t
        r = pl.ds(pl.multiple_of(t * LANES, LANES), LANES)
        o = pl.ds(pl.multiple_of(me * ROWS + t * LANES, LANES), LANES)
        out[k, :, o] = (lat[k, :, r] * spread[k]).astype(BF16)
        by_plus(j).start()
        by_minus(j).start()
        across(OWN, j).start()

    for k in range(2):
        spread_out(k)

        def make_step(t, _):
            make(k, t)
            return 0

        lax.fori_loop(0, STRIPS, make_step, 0)

    col[...] = jnp.concatenate(
        [jnp.concatenate([column[0:1], column[1:2], column[2:3], column[3:4]], axis=1),
         jnp.concatenate([column[4:5], column[5:6], column[6:7],
                          pltpu.roll(column, LANES - TAIL, axis=1)[3:4]], axis=1)], axis=0)

    row7 = jnp.concatenate([sums[8 * s + 7:8 * s + 8, :] for s in range(GROUP)], axis=0)
    lane8 = lax.broadcasted_iota(jnp.int32, (8, LANES), 1)
    for t in range(5):
        place = lane8 + LANES * t
        here = (place >= cols * PER) & (place < cols * PER + PER)
        ny[0, :, LANES * t:LANES * t + LANES] = jnp.where(here, row7, 0.0)

    def y_copy(src, dst, k, dev):
        return pltpu.make_async_remote_copy(
            src_ref=ny.at[src], dst_ref=ny.at[dst], send_sem=y_send.at[k], recv_sem=y_recv.at[k],
            device_id=dev, device_id_type=MESH)

    to_up, to_down, onward = y_copy(0, 1, 0, at_y(1)), y_copy(0, 2, 1, at_y(NY - 1)), y_copy(1, 3, 2, at_y(1))

    def z_right(src, s):
        return pltpu.make_async_remote_copy(
            src_ref=src, dst_ref=zr.at[s], send_sem=zr_send.at[s], recv_sem=zr_recv.at[s],
            device_id=at_z(1), device_id_type=MESH)

    def z_left(src, s):
        return pltpu.make_async_remote_copy(
            src_ref=src, dst_ref=zl.at[s], send_sem=zl_send.at[s], recv_sem=zl_recv.at[s],
            device_id=at_z(NZ - 1), device_id_type=MESH)

    to_up.start()
    to_down.start()

    def even(j):
        by_plus(j, source[LEFT]).wait_recv()
        onward_plus(j).start()
        across(LEFT, j).start()
        by_minus(j, source[RIGHT]).wait_recv()
        across(RIGHT, j).start()

    def odd(j):
        by_minus(j, source[RIGHT]).wait_recv()
        onward_minus(j).start()
        across(RIGHT, j).start()
        by_plus(j, source[LEFT]).wait_recv()
        across(LEFT, j).start()

    even(0)
    to_up.wait_recv()
    onward.start()
    odd(1)
    to_down.wait_recv()
    onward.wait_recv()
    onward.wait_send()
    to_up.wait_send()
    to_down.wait_send()
    ny[0] = ny[0] + ny[1] + (ny[2] + ny[3])
    z_right(ny.at[0], 0).start()
    z_left(ny.at[0], 0).start()

    def pair(q, _):
        s = 2 * q - 1
        even(2 * q)
        z_right(ny.at[0], s - 1).wait_recv()
        z_right(zr.at[s - 1], s).start()
        z_left(ny.at[0], s - 1).wait_recv()

        @pl.when(q < PAIRS - 1)
        def _():
            z_left(zl.at[s - 1], s).start()

        odd(2 * q + 1)
        z_right(ny.at[0], s).wait_recv()

        @pl.when(q < PAIRS - 1)
        def _():
            z_right(zr.at[s], s + 1).start()
            z_left(ny.at[0], s).wait_recv()
            z_left(zl.at[s], s + 1).start()

        return 0

    lax.fori_loop(1, PAIRS, pair, 0)

    gain = ny[0]
    for s in range(8):
        gain = gain + zr[s]
    for s in range(7):
        gain = gain + zl[s]
    for t in range(5):
        nscr[pl.ds(t, 8, stride=5), :] = gain[:, LANES * t:LANES * t + LANES]
    norm[...] = nscr[...].astype(BF16)

    def far_step(j, _):
        onward_plus(j, source[FAR]).wait_recv()
        across(FAR, j).start()
        return 0

    lax.fori_loop(0, NCH, far_step, 0)

    for k, peer in enumerate(group):
        sum_copy(k, peer, me).wait_send()

    def drain_z(s, _):
        z_right(ny.at[0], s).wait_send()

        @pl.when(s < 7)
        def _():
            z_left(ny.at[0], s).wait_send()

        return 0

    lax.fori_loop(0, 8, drain_z, 0)

    def drain_step(j, _):
        by_plus(j).wait_send()
        by_minus(j).wait_send()
        onward_plus(j).wait_send()
        for k in range(4):
            across(k, j).wait_send()
            across(k, j, twin).wait_recv()
        return 0

    lax.fori_loop(0, NCH, drain_step, 0)


def write_kernel(both, gate, up, sem):
    copies = []
    for k, dst in enumerate((gate, up)):
        for q in range(5):
            r = pl.ds(q * STEP, STEP)
            copies.append(pltpu.make_async_copy(both.at[k, r, :], dst.at[r, :], sem.at[5 * k + q]))
    for copy in copies:
        copy.start()
    for copy in copies:
        copy.wait()


def on_device(tg, lg, hg, tu, lu, hu, nt, ns):
    dma = pltpu.SemaphoreType.DMA
    hbm = pl.BlockSpec(memory_space=pltpu.HBM)
    vmem = pl.BlockSpec(memory_space=pltpu.VMEM)
    both, col, norm = pl.pallas_call(
        gather_kernel,
        name="gather_weights",
        out_shape=(
            pltpu.VMEM((2, WIDE, D_MODEL), BF16),
            jax.ShapeDtypeStruct((2, 512), F32),
            jax.ShapeDtypeStruct((NORM_ROWS, LANES), BF16),
        ),
        in_specs=[hbm] * 8,
        out_specs=(vmem, vmem, vmem),
        scratch_shapes=[
            pltpu.VMEM((2, WIDE, ROWS), BF16), pltpu.VMEM((2, RANK, ROWS), BF16),
            pltpu.VMEM((2, RANK, WIDE), BF16), pltpu.VMEM((2, WIDE, RANK), BF16),
            pltpu.SMEM((PER,), F32), pltpu.SMEM((PER,), F32),
            pltpu.VMEM((2, WIDE, ROWS), F32), pltpu.VMEM((7 * LANES, LANES), F32),
            pltpu.VMEM((2, WIDE, LANES), F32), pltpu.VMEM((GROUP * 8, LANES), F32),
            pltpu.VMEM((4, 8, 640), F32), pltpu.VMEM((8, 8, 640), F32), pltpu.VMEM((7, 8, 640), F32),
            pltpu.VMEM((NORM_ROWS, LANES), F32),
            dma((8,)), dma((GROUP - 1,)), dma((GROUP,)),
            dma((NCH,)), dma((NCH,)), dma((NCH,)), dma((NCH,)), dma((NCH,)), dma((NCH,)),
            dma((4 * NCH,)), dma((4 * NCH,)),
            dma((3,)), dma((4,)), dma((8,)), dma((8,)), dma((7,)), dma((7,)),
        ],
        compiler_params=pltpu.CompilerParams(
            collective_id=0, has_side_effects=True, vmem_limit_bytes=24 << 20),
    )(*(pltpu.with_memory_space_constraint(a, pltpu.HBM) for a in (tg.T, lg.T, hg, tu.T, lu.T, hu, nt, ns)))
    gate, up = pl.pallas_call(
        write_kernel,
        name="write_weights",
        out_shape=(jax.ShapeDtypeStruct((WIDE, D_MODEL), BF16),) * 2,
        in_specs=[vmem],
        out_specs=(hbm, hbm),
        scratch_shapes=[dma((10,))],
        compiler_params=pltpu.CompilerParams(vmem_limit_bytes=4 << 20),
    )(pltpu.with_memory_space_constraint(both, pltpu.VMEM))
    return gate.T, up.T, col[0, :WIDE], col[1, :WIDE], norm.reshape(D_MODEL)


def solution(mesh):
    return jax.shard_map(
        on_device,
        mesh=mesh,
        in_specs=(
            P("zero", "cols"), P("zero", None), P(None, "cols"),
            P("zero", "cols"), P("zero", None), P(None, "cols"),
            P(("zero", "cols")), P(("zero", "cols")),
        ),
        out_specs=(P(None, "cols"), P(None, "cols"), P("cols"), P("cols"), P()),
        check_vma=False,
    )
```

time: 96 us -> 60.3 us (0.63)
  blocking collectives: 67.1 us -> 0 us
  Pallas kernels: 0 us -> 58.4 us
  between operations: 14.8 us -> 0.65 us
  local copies, waits for them, and re-layouts: 9.18 us -> 1.19 us
  matrix products: 3.18 us -> 0 us
  other arithmetic: 1.38 us -> 0 us
    pallas_call x0 -> x2, Pallas kernels: none -> 58.4 us  [the longest x1 55 us: on_device(): pl.pallas_call(gather_kernel, name='gather_weights', out_shape=(pltpu.VME...]
    all_gather x3 -> x0, blocking collectives: 46.4 us -> none  [stacked_from(): parts = lax.all_gather(parts, axes[k], axis=0, tiled=True)]
    all_to_all x1 -> x0, blocking collectives: 13.9 us -> none  [from_everyone(): return lax.all_to_all(copies, axis, split_axis=0, concat_axis=0, tiled=True)]
    unnamed x1 -> x0, blocking collectives: 6.85 us -> none
    split x1 -> x0, local copies, waits for them, and re-layouts: 5.78 us -> none  [in_one_piece(): jnp.split(result, [sum(widths[:k]) for k in range(1, len(widths))], axis=...]
    dot_general x2 -> x0, matrix products: 3.18 us -> none  [the longest x1 1.62 us: on_device(): jnp.dot(low_up, high_up, preferred_element_type=jnp.float32)]
    unnamed x14 -> x1, local copies, waits for them, and re-layouts: 2.46 us -> 0.6 us
    concatenate x2 -> x0, other arithmetic: 1.13 us -> none  [the longest x1 1.05 us: in_one_piece(): both = jnp.concatenate(arrays, axis=along)]
  transfers between devices with their start and end apart: 1 -> 0, of which waited for: 0 -> 0; matrix products, arithmetic and copies ran while one was open for 3% -> 0% of each run, Pallas kernels for 0% -> 0%
where the time goes in v1:
time: 60.3 us; the launch traced here: 60.2 us
  Pallas kernels  58.4 us (97%)
  local copies, waits for them, and re-layouts  1.19 us (2%)
  between operations  0.65 us (1%)
    pallas_call x1, Pallas kernels, on_device(): pl.pallas_call(gather_kernel, name='gather_weights', out_shape=(pltpu.VME...  55 us
    pallas_call x1, Pallas kernels, on_device(): pl.pallas_call(write_kernel, name='write_weights', out_shape=(jax.ShapeDt...  3.34 us

profile of v1, /device:TPU:1, one launch (start us, length us, event | category | flops | bytes accessed | tf_op | source)
XLA Modules:
  0.0 60.2 jit_solution(10723243326928527720)
XLA Ops:
  0.6 55.0 %gather_weights.1 = (bf16[2,400,5120]{2,1,0:T(8,128)(2,1)S(1)}, f32[2,512]{1,0:T(2,128)S(1)}, bf16[40,128]{1,0:T(8,128)(2,1)S(1)}) custom-call(bf16[400,640]{1,0:T(8,128)(2,1)} %bitcast.10, bf16[64,640]{1,0:T(8,128)(2,1)} %bitcast.12, bf16[64,400]{1,0:T(8,128)(2,1)} %hg.1, bf16[400,640]{1,0:T(8,128)(2,1)} %bitcast.11, bf16[64,640]{1,0:T(8,128)(2,1)} %bitcast.13, ...), custom_call_target="tpu_custom_call" | custom-call | tf_op jit(solution)/shard_map/gather_weights/pallas_call | solution.py:328
  55.7 3.3 %write_weights.1 = (bf16[400,5120]{1,0:T(8,128)(2,1)}, bf16[400,5120]{1,0:T(8,128)(2,1)}) custom-call(bf16[2,400,5120]{2,1,0:T(8,128)(2,1)S(1)} %get-tuple-element.10.both), custom_call_target="tpu_custom_call" | custom-call | tf_op jit(solution)/shard_map/write_weights/pallas_call | solution.py:354
  59.0 0.6 fusion
  59.6 0.6 copy.14

commit v2 on v0

v2 whole, which is shorter than its diff:
```python
import jax
import jax.numpy as jnp
from jax import lax
from jax.experimental import pallas as pl
from jax.experimental.pallas import tpu as pltpu
from jax.sharding import PartitionSpec as P

F32, BF16 = jnp.float32, jnp.bfloat16
MESH = pl.DeviceIdType.MESH

NX, NC, NY, NZ = 4, 2, 4, 16
GROUP = NX * NC
D_MODEL, WIDE, RANK = 5120, 400, 64
ROWS = D_MODEL // GROUP
LANES = 128
STRIPS = ROWS // LANES
MAIN, TAIL = 384, 16
STEP = 80
PER = 10
NORM_ROWS = D_MODEL // LANES

RAW = range(0, STRIPS)
LOW = range(STRIPS, STRIPS + 2)
UP = range(STRIPS + 2, 2 * STRIPS + 2)
PIECES = 2 * STRIPS + 2
BY_PLUS = (0, 2, 4, 5, 8, 10)
OWN, LEFT, RIGHT, FAR = 0, 1, 2, 3


def gather_kernel(
    tg, lg, hg, tu, lu, hu, nt, ns,
    out_g, out_u, col_g, col_u, norm,
    raw, low, tuv, luv, hv, ht, ntv, nsv,
    lat, part, spread, sums, ybuf, zbuf, gains, nscr,
    load_sem, here, y_token, z_token,
    sum_send, sum_recv, sum_d_send, sum_d_recv,
    p_send, m_send, f_send, l_recv, r_recv, o_recv, d_send, d_recv,
    y_send, y_recv, z_send, z_recv, g_send, g_recv,
):
    me = lax.axis_index("zero")
    cols = lax.axis_index("cols")
    x, c = me // NC, me % NC
    z, y = cols // NY, cols % NY

    def chip(dx, core):
        return ((x + dx) % NX) * NC + core

    def at_x(dx, core):
        return (chip(dx, core), cols)

    def at_y(dy):
        return (me, z * NY + (y + dy) % NY)

    def at_z(dz):
        return (me, ((z + dz) % NZ) * NY + y)

    def signal(sem, dev):
        pl.semaphore_signal(sem, inc=1, device_id=dev, device_id_type=MESH)

    def copy_to(src, dst, send, recv, dev):
        return pltpu.make_async_remote_copy(
            src_ref=src, dst_ref=dst, send_sem=send, recv_sem=recv,
            device_id=dev, device_id_type=MESH)

    def remote(ref, send, recv, dev):
        return copy_to(ref, ref, send, recv, dev)

    partner = at_x(0, 1 - c)
    plus, minus, far = at_x(1, c), at_x(NX - 1, c), at_x(2, c)
    rail = [plus, minus, far]

    def lanes(shard, at=0, n=ROWS):
        return pl.ds(pl.multiple_of(shard * ROWS + at, LANES), n)

    mine = lanes(me)

    loads = [
        pltpu.make_async_copy(a, b, load_sem.at[i])
        for i, (a, b) in enumerate(
            ((tg, raw.at[:, mine]), (hg, hv.at[0]), (lg, low.at[:, mine]),
             (hu, hv.at[1]), (lu, luv), (tu, tuv), (nt, ntv), (ns, nsv))
        )
    ]
    for load in loads:
        load.start()

    barrier = pltpu.get_barrier_semaphore()
    for peer in rail:
        signal(barrier, peer)

    @pl.when(c == 1)
    def _():
        for peer in (partner, at_y(1), at_y(NY - 1), at_z(1), at_z(NZ - 1)):
            signal(barrier, peer)

    source = [me, chip(NX - 1, c), chip(1, c), chip(2, c)]
    twin = [chip(0, 1 - c), chip(NX - 1, 1 - c), chip(1, 1 - c), chip(2, 1 - c)]

    def piece(shard, n):
        if n in RAW:
            return raw.at[:, lanes(shard, n * LANES, LANES)]
        if n in LOW:
            return low.at[pl.ds((n - STRIPS) * (RANK // 2), RANK // 2), lanes(shard)]
        return out_u.at[:, lanes(shard, (n - STRIPS - 2) * LANES, LANES)]

    def by_plus(n, k=OWN):
        return remote(piece(source[k], n), p_send.at[n], l_recv.at[n], plus)

    def by_minus(n, k=OWN):
        return remote(piece(source[k], n), m_send.at[n], r_recv.at[n], minus)

    def onward(n, k=None):
        k, dev = (LEFT if k is None else k, plus) if n in BY_PLUS else (RIGHT if k is None else k, minus)
        return remote(piece(source[k], n), f_send.at[n], o_recv.at[n], dev)

    def across(k, n, shards=source):
        i = k * PIECES + n
        return remote(piece(shards[k], n), d_send.at[i], d_recv.at[i], partner)

    def both_ways(n):
        by_plus(n).start()
        by_minus(n).start()

    def pass_on(n):
        def from_left():
            by_plus(n, LEFT).wait_recv()
            if n in BY_PLUS:
                onward(n).start()
            across(LEFT, n).start()

        def from_right():
            by_minus(n, RIGHT).wait_recv()
            if n not in BY_PLUS:
                onward(n).start()
            across(RIGHT, n).start()

        for step in (from_left, from_right) if n in BY_PLUS else (from_right, from_left):
            step()

    loads[0].wait()
    pl.semaphore_wait(barrier, 4 + 3 * c)
    both_ways(0)

    @pl.when(c == 0)
    def _():
        signal(here, partner)

    @pl.when(c == 1)
    def _():
        for peer in (at_y(1), at_y(NY - 1)):
            signal(y_token, peer)
        for peer in (at_z(1), at_z(NZ - 1)):
            signal(z_token.at[0], peer)

    def dot(a, b):
        return jnp.dot(a, b, preferred_element_type=F32)

    loads[1].wait()
    loads[3].wait()
    for k in range(2):
        ht[k] = (hv[k].astype(F32).T * 2.0).astype(BF16)
    part[WIDE + TAIL:512, :] = jnp.zeros((512 - WIDE - TAIL, LANES), F32)

    for k in range(2):
        loads[2 + 2 * k].wait()
        if k == 1:
            loads[5].wait()
        for q in range(WIDE // STEP):
            r = slice(STEP * q, STEP * q + STEP)
            if k == 0:
                w = raw[r, mine].astype(F32) + dot(ht[0, r, :], low[:, mine])
            else:
                w = tuv[r, :].astype(F32) + dot(ht[1, r, :], luv[...])
                lat[r, :] = w
            w = w * w
            s = w[:, 0:LANES]
            for t in range(1, STRIPS):
                s = s + w[:, LANES * t:LANES * t + LANES]
            if k == 0:
                part[r, :] = s
            elif r.stop <= MAIN:
                part[512 + r.start:512 + r.stop, :] = s
            else:
                part[512 + r.start:512 + MAIN, :] = s[:MAIN - r.start]
                part[WIDE:WIDE + TAIL, :] = s[MAIN - r.start:]
    loads[6].wait()
    loads[7].wait()

    lane = lax.broadcasted_iota(jnp.int32, (1, LANES), 1)
    own_gains = jnp.zeros((1, LANES), F32)
    for k in range(PER):
        own_gains = jnp.where(lane == (cols * PER + k) % LANES, ntv[k] + nsv[k], own_gains)

    sums[me] = jnp.concatenate(
        [jnp.sum(part[LANES * t:LANES * t + LANES, :].T, axis=0, keepdims=True) for t in range(7)]
        + [own_gains], axis=0)

    def sum_copy(i, peer, owner):
        return remote(sums.at[owner], sum_send.at[i], sum_recv.at[i], peer)

    def sum_across(k, owners=source):
        return remote(sums.at[owners[k]], sum_d_send.at[k], sum_d_recv.at[k], partner)

    for i, peer in enumerate(rail):
        sum_copy(i, peer, me).start()
    for n in (*LOW, *RAW[1:]):
        both_ways(n)

    @pl.when(c == 1)
    def _():
        pl.semaphore_wait(here, 1)

    sum_across(OWN).start()
    for n in (*RAW, *LOW):
        across(OWN, n).start()

    pass_on(0)
    for i, k in enumerate((LEFT, RIGHT, FAR)):
        sum_copy(i, plus, source[k]).wait_recv()
        sum_across(k).start()

    @pl.when(c == 1)
    def _():
        pl.semaphore_wait(z_token.at[0], 2)
        for peer in (at_z(2), at_z(NZ - 2)):
            signal(z_token.at[1], peer)
        pl.semaphore_wait(y_token, 2)

    for n in (*LOW, *RAW[1:]):
        pass_on(n)

    for k in range(4):
        sum_across(k, twin).wait_recv()

    total = sums[0]
    for s in range(1, GROUP):
        total = total + sums[s]
    column = jnp.sqrt(total)
    inverse = jnp.concatenate([1.0 / column, jnp.zeros((LANES - 8, LANES), F32)], axis=0).T

    def spread_out(k):
        for t in range(3):
            spread[k, LANES * t:LANES * t + LANES, :] = jnp.broadcast_to(
                inverse[:, 4 * k + t:4 * k + t + 1], (LANES, LANES))
        spread[k, MAIN:, :] = jnp.broadcast_to(
            inverse[TAIL * k:TAIL * k + TAIL, 3:4], (TAIL, LANES))

    spread_out(1)
    for n in UP:
        t = n - STRIPS - 2
        out_u[:, lanes(me, t * LANES, LANES)] = (lat[:, t * LANES:t * LANES + LANES] * spread[1]).astype(BF16)
        both_ways(n)
        across(OWN, n).start()
    spread_out(0)

    col_g[...] = jnp.concatenate(
        [column[0:1], column[1:2], column[2:3], column[3:4]], axis=1)[:, :WIDE]
    col_u[...] = jnp.concatenate(
        [column[4:5], column[5:6], column[6:7], pltpu.roll(column, LANES - TAIL, axis=1)[3:4]], axis=1)[:, :WIDE]

    y_copies = [copy_to(ybuf.at[0], ybuf.at[i + 1], y_send.at[i], y_recv.at[i], at_y(dy))
                for i, dy in enumerate((1, NY - 1, 2))]

    def z_copy(d):
        return copy_to(zbuf.at[0], zbuf.at[d], z_send.at[d - 1], z_recv.at[d - 1], at_z(d))

    @pl.when(c == 1)
    def _():
        ybuf[0] = jnp.concatenate([sums[s][7:8, :] for s in range(GROUP)], axis=0)
        for copy in y_copies:
            copy.start()
        pl.semaphore_wait(z_token.at[1], 2)
        for peer in (at_z(4), at_z(NZ - 4)):
            signal(z_token.at[2], peer)

    for n in (*RAW[:1], *LOW, *RAW[1:]):
        onward(n, FAR).wait_recv()
        across(FAR, n).start()

    @pl.when(c == 1)
    def _():
        for copy in y_copies:
            copy.wait_recv()
        zbuf[0] = (ybuf[0] + ybuf[1]) + (ybuf[2] + ybuf[3])
        pl.semaphore_wait(z_token.at[2], 2)
        for d in range(1, NZ):
            z_copy(d).start()

    for n in (*RAW, *LOW):
        for k in range(4):
            across(k, n, twin).wait_recv()

    def finish(i, _):
        w = pl.ds(pl.multiple_of(i * 2 * LANES, 2 * LANES), 2 * LANES)
        for q in range(WIDE // STEP):
            r = slice(STEP * q, STEP * q + STEP)
            s = spread[0, r, :]
            v = raw[r, w].astype(F32) + dot(ht[0, r, :], low[:, w])
            out_g[r, w] = (v * jnp.concatenate([s, s], axis=1)).astype(BF16)
        return 0

    lax.fori_loop(0, D_MODEL // (2 * LANES), finish, 0)

    for n in UP:
        pass_on(n)
    for n in UP[:-2]:
        onward(n, FAR).wait_recv()
        across(FAR, n).start()

    def gains_across():
        return remote(gains, g_send.at[0], g_recv.at[0], partner)

    @pl.when(c == 1)
    def _():
        for d in range(1, NZ):
            z_copy(d).wait_recv()
        lane8 = lax.broadcasted_iota(jnp.int32, (8, LANES), 1)
        tiles = [jnp.zeros((8, LANES), F32) for _ in range(5)]
        for d in range(NZ):
            start = ((z + NZ - d) % NZ) * NY * PER
            tile = zbuf[d]
            for t in range(5):
                place = lane8 + LANES * t
                tiles[t] = jnp.where((place >= start) & (place < start + NY * PER), tile, tiles[t])
        for t in range(5):
            gains[:, LANES * t:LANES * t + LANES] = tiles[t]
        gains_across().start()

    for n in UP[-2:]:
        onward(n, FAR).wait_recv()
        across(FAR, n).start()

    @pl.when(c == 0)
    def _():
        gains_across().wait_recv()

    for t in range(5):
        nscr[pl.ds(t, 8, stride=5), :] = gains[:, LANES * t:LANES * t + LANES]
    norm[...] = nscr[...].astype(BF16)

    @pl.when(c == 1)
    def _():
        gains_across().wait_send()
        for copy in y_copies:
            copy.wait_send()
        for d in range(1, NZ):
            z_copy(d).wait_send()

    for i, peer in enumerate(rail):
        sum_copy(i, peer, me).wait_send()
    for k in range(4):
        sum_across(k).wait_send()
    for n in range(PIECES):
        by_plus(n).wait_send()
        by_minus(n).wait_send()
        onward(n).wait_send()
        for k in range(4):
            across(k, n).wait_send()
            if n in UP:
                across(k, n, twin).wait_recv()


def write_kernel(*refs):
    n = (len(refs) - 1) // 2
    sources, targets, sem = refs[:n], refs[n:2 * n], refs[2 * n]
    copies = []
    for src, dst in zip(sources, targets):
        tall = src.shape[0] == WIDE
        for q in range(WIDE // STEP if tall else 1):
            r = pl.ds(q * STEP, STEP) if tall else slice(None)
            copies.append(pltpu.make_async_copy(src.at[r, :], dst.at[r, :], sem.at[len(copies)]))
    for copy in copies:
        copy.start()
    for copy in copies:
        copy.wait()


def on_device(tg, lg, hg, tu, lu, hu, nt, ns):
    dma, regular = pltpu.SemaphoreType.DMA, pltpu.SemaphoreType.REGULAR
    hbm = pl.BlockSpec(memory_space=pltpu.HBM)
    vmem = pl.BlockSpec(memory_space=pltpu.VMEM)
    results = (
        ((WIDE, D_MODEL), BF16), ((WIDE, D_MODEL), BF16),
        ((1, WIDE), F32), ((1, WIDE), F32), ((NORM_ROWS, LANES), BF16),
    )
    made = pl.pallas_call(
        gather_kernel,
        name="gather_weights",
        out_shape=tuple(pltpu.VMEM(*r) for r in results),
        in_specs=[hbm] * 8,
        out_specs=(vmem,) * 5,
        scratch_shapes=[
            pltpu.VMEM((WIDE, D_MODEL), BF16), pltpu.VMEM((RANK, D_MODEL), BF16),
            pltpu.VMEM((WIDE, ROWS), BF16), pltpu.VMEM((RANK, ROWS), BF16),
            pltpu.VMEM((2, RANK, WIDE), BF16), pltpu.VMEM((2, WIDE, RANK), BF16),
            pltpu.SMEM((PER,), F32), pltpu.SMEM((PER,), F32),
            pltpu.VMEM((WIDE, ROWS), F32), pltpu.VMEM((7 * LANES, LANES), F32),
            pltpu.VMEM((2, WIDE, LANES), F32), pltpu.VMEM((GROUP, 8, LANES), F32),
            pltpu.VMEM((NY, 8, LANES), F32), pltpu.VMEM((NZ, 8, LANES), F32),
            pltpu.VMEM((8, 5 * LANES), F32), pltpu.VMEM((NORM_ROWS, LANES), F32),
            dma((8,)), regular, regular, regular((3,)),
            dma((3,)), dma((3,)), dma((4,)), dma((4,)),
            *[dma((PIECES,))] * 6, dma((4 * PIECES,)), dma((4 * PIECES,)),
            dma((3,)), dma((3,)), dma((NZ - 1,)), dma((NZ - 1,)), dma((1,)), dma((1,)),
        ],
        compiler_params=pltpu.CompilerParams(
            collective_id=0, has_side_effects=True, vmem_limit_bytes=24 << 20),
    )(*(pltpu.with_memory_space_constraint(a, pltpu.HBM) for a in (tg.T, lg.T, hg, tu.T, lu.T, hu, nt, ns)))
    gate, up, col_g, col_u, norm = pl.pallas_call(
        write_kernel,
        name="write_results",
        out_shape=tuple(jax.ShapeDtypeStruct(*r) for r in results),
        in_specs=[vmem] * 5,
        out_specs=(hbm,) * 5,
        scratch_shapes=[dma((13,))],
        compiler_params=pltpu.CompilerParams(vmem_limit_bytes=4 << 20),
    )(*(pltpu.with_memory_space_constraint(a, pltpu.VMEM) for a in made))
    return gate.T, up.T, col_g.reshape(WIDE), col_u.reshape(WIDE), norm.reshape(D_MODEL)


def solution(mesh):
    return jax.shard_map(
        on_device,
        mesh=mesh,
        in_specs=(
            P("zero", "cols"), P("zero", None), P(None, "cols"),
            P("zero", "cols"), P("zero", None), P(None, "cols"),
            P(("zero", "cols")), P(("zero", "cols")),
        ),
        out_specs=(P(None, "cols"), P(None, "cols"), P("cols"), P("cols"), P()),
        check_vma=False,
    )
```

time: 96 us -> 54.7 us (0.57)
  blocking collectives: 67.1 us -> 0 us
  Pallas kernels: 0 us -> 53.9 us
  between operations: 14.8 us -> 0.64 us
  local copies, waits for them, and re-layouts: 9.18 us -> 0 us
  matrix products: 3.18 us -> 0 us
  other arithmetic: 1.38 us -> 0 us
    pallas_call x0 -> x2, Pallas kernels: none -> 53.9 us  [the longest x1 50.6 us: on_device(): pl.pallas_call(gather_kernel, name='gather_weights', out_shape=tuple((plt...]
    all_gather x3 -> x0, blocking collectives: 46.4 us -> none  [stacked_from(): parts = lax.all_gather(parts, axes[k], axis=0, tiled=True)]
    all_to_all x1 -> x0, blocking collectives: 13.9 us -> none  [from_everyone(): return lax.all_to_all(copies, axis, split_axis=0, concat_axis=0, tiled=True)]
    unnamed x1 -> x0, blocking collectives: 6.85 us -> none
    split x1 -> x0, local copies, waits for them, and re-layouts: 5.78 us -> none  [in_one_piece(): jnp.split(result, [sum(widths[:k]) for k in range(1, len(widths))], axis=...]
    dot_general x2 -> x0, matrix products: 3.18 us -> none  [the longest x1 1.62 us: on_device(): jnp.dot(low_up, high_up, preferred_element_type=jnp.float32)]
    unnamed x14 -> x0, local copies, waits for them, and re-layouts: 2.46 us -> none
    concatenate x2 -> x0, other arithmetic: 1.13 us -> none  [the longest x1 1.05 us: in_one_piece(): both = jnp.concatenate(arrays, axis=along)]
  transfers between devices with their start and end apart: 1 -> 0, of which waited for: 0 -> 0; matrix products, arithmetic and copies ran while one was open for 3% -> 0% of each run, Pallas kernels for 0% -> 0%
where the time goes in v2:
time: 54.7 us; the launch traced here: 54.6 us
  Pallas kernels  53.9 us (99%)
  between operations  0.64 us (1%)
    pallas_call x1, Pallas kernels, on_device(): pl.pallas_call(gather_kernel, name='gather_weights', out_shape=tuple((plt...  50.6 us
    pallas_call x1, Pallas kernels, on_device(): pl.pallas_call(write_kernel, name='write_results', out_shape=tuple((jax.S...  3.37 us

profile of v2, /device:TPU:1, one launch (start us, length us, event | category | flops | bytes accessed | tf_op | source)
XLA Modules:
  0.0 54.6 jit_solution(6312577717933275422)
XLA Ops:
  0.6 50.6 %gather_weights.1 = (bf16[400,5120]{1,0:T(8,128)(2,1)S(1)}, bf16[400,5120]{1,0:T(8,128)(2,1)S(1)}, f32[1,400]{1,0:T(1,128)S(1)}, f32[1,400]{1,0:T(1,128)S(1)}, bf16[40,128]{1,0:T(8,128)(2,1)S(1)}) custom-call(bf16[400,640]{1,0:T(8,128)(2,1)} %bitcast.9, bf16[64,640]{1,0:T(8,128)(2,1)} %bitcast.11, bf16[64,400]{1,0:T(8,128)(2,1)} %hg.1, ...), custom_call_target="tpu_custom_call" | custom-call | tf_op jit(solution)/shard_map/gather_weights/pallas_call | solution.py:386
  51.2 3.4 %write_results.1 = (bf16[400,5120]{1,0:T(8,128)(2,1)}, bf16[400,5120]{1,0:T(8,128)(2,1)}, f32[1,400]{1,0:T(1,128)}, f32[1,400]{1,0:T(1,128)}, bf16[40,128]{1,0:T(8,128)(2,1)}) custom-call(bf16[400,5120]{1,0:T(8,128)(2,1)S(1)} %get-tuple-element.15.refs_0_, bf16[400,5120]{1,0:T(8,128)(2,1)S(1)} %get-tuple-element.16.refs_1_, ...), custom_call_target="tpu_custom_call" | custom-call | tf_op jit(solution)/shard_map/write_results/pallas_call | solution.py:409

commit v3 on v2

v3 whole, which is shorter than its diff:
```python
import jax
import jax.numpy as jnp
from jax import lax
from jax.experimental import pallas as pl
from jax.experimental.pallas import tpu as pltpu
from jax.sharding import PartitionSpec as P

F32, BF16 = jnp.float32, jnp.bfloat16
MESH = pl.DeviceIdType.MESH

NX, NC, NY, NZ = 4, 2, 4, 16
GROUP = NX * NC
D_MODEL, WIDE, RANK = 5120, 400, 64
ROWS = D_MODEL // GROUP
LANES = 128
STRIPS = ROWS // LANES
MAIN, TAIL = 384, 16
STEP = 80
PER = 10
NORM_ROWS = D_MODEL // LANES

RAW = range(0, STRIPS)
LOW = range(STRIPS, STRIPS + 2)
UP = range(STRIPS + 2, 2 * STRIPS + 2)
PIECES = 2 * STRIPS + 2
BY_PLUS = (0, 2, 4, 5, 8, 10)
OWN, LEFT, RIGHT, FAR = 0, 1, 2, 3


def gather_kernel(
    tg, lg, hg, tu, lu, hu, nt, ns,
    out_g, out_u, col_g, col_u, norm,
    raw, low, tuv, luv, hv, ht, ntv, nsv,
    lat, part, spread, sums, gbuf, ybuf, zbuf, nscr,
    load_sem, here, y_token, z_token,
    send, l_recv, r_recv, far_recv, d_recv, small_recv, n_send,
):
    me = lax.axis_index("zero")
    cols = lax.axis_index("cols")
    x, c = me // NC, me % NC
    z, y = cols // NY, cols % NY

    def chip(dx, core):
        return ((x + dx) % NX) * NC + core

    def at_x(dx, core):
        return (chip(dx, core), cols)

    def at_y(dy):
        return (me, z * NY + (y + dy) % NY)

    def at_z(dz):
        return (me, ((z + dz) % NZ) * NY + y)

    def signal(sem, dev):
        pl.semaphore_signal(sem, inc=1, device_id=dev, device_id_type=MESH)

    def copy_to(src, dst, send, recv, dev):
        return pltpu.make_async_remote_copy(
            src_ref=src, dst_ref=dst, send_sem=send, recv_sem=recv,
            device_id=dev, device_id_type=MESH)

    def remote(ref, send, recv, dev):
        return copy_to(ref, ref, send, recv, dev)

    partner = at_x(0, 1 - c)
    plus, minus, far = at_x(1, c), at_x(NX - 1, c), at_x(2, c)
    rail = [plus, minus, far]

    def lanes(shard, at=0, n=ROWS):
        return pl.ds(pl.multiple_of(shard * ROWS + at, LANES), n)

    mine = lanes(me)

    head = me == 0
    barrier = pltpu.get_barrier_semaphore()
    for peer in rail:
        signal(barrier, peer)

    @pl.when(c == 1)
    def _():
        signal(barrier, partner)

    loads = [
        pltpu.make_async_copy(a, b, load_sem.at[i])
        for i, (a, b) in enumerate(
            ((tg, raw.at[:, mine]), (nt, ntv), (ns, nsv), (hg, hv.at[0]), (lg, low.at[:, mine]),
             (hu, hv.at[1]), (lu, luv), (tu, tuv))
        )
    ]
    for load in loads:
        load.start()

    for dy in (1, NY - 1):
        @pl.when(head & (y != 0))
        def _(dy=dy):
            signal(barrier, at_y(dy))

    for dz in (1, NZ - 1):
        @pl.when(head & ((z + dz) % NZ != 0))
        def _(dz=dz):
            signal(barrier, at_z(dz))

    source = [me, chip(NX - 1, c), chip(1, c), chip(2, c)]

    def piece(shard, n):
        if n in RAW:
            return raw.at[:, lanes(shard, n * LANES, LANES)]
        if n in LOW:
            return low.at[pl.ds((n - STRIPS) * (RANK // 2), RANK // 2), lanes(shard)]
        return out_u.at[:, lanes(shard, (n - STRIPS - 2) * LANES, LANES)]

    def sent(n):
        return send.at[0 if n in RAW else 1 if n in LOW else 2]

    def by_plus(n, k=OWN):
        return remote(piece(source[k], n), sent(n), l_recv.at[n], plus)

    def by_minus(n, k=OWN):
        return remote(piece(source[k], n), sent(n), r_recv.at[n], minus)

    def onward(n, k=None):
        k, dev = (LEFT if k is None else k, plus) if n in BY_PLUS else (RIGHT if k is None else k, minus)
        return remote(piece(source[k], n), sent(n), far_recv.at[0 if n in RAW else 1 if n in LOW else n - STRIPS], dev)

    def across(k, n):
        kind = (0 if n in RAW else 1) + (2 if k == FAR else 0) if n not in UP else 4
        return remote(piece(source[k], n), sent(n), d_recv.at[kind], partner)

    def crossed(ref, kind):
        return remote(ref, send.at[0], d_recv.at[kind], partner)

    def both_ways(n):
        by_plus(n).start()
        by_minus(n).start()

    def pass_on(n, now=True):
        def from_left():
            by_plus(n, LEFT).wait_recv()
            if n in BY_PLUS:
                onward(n).start()
            if now:
                across(LEFT, n).start()

        def from_right():
            by_minus(n, RIGHT).wait_recv()
            if n not in BY_PLUS:
                onward(n).start()
            if now:
                across(RIGHT, n).start()

        for step in (from_left, from_right) if n in BY_PLUS else (from_right, from_left):
            step()

    loads[1].wait()
    loads[2].wait()
    row8 = lax.broadcasted_iota(jnp.int32, (8, LANES), 0)
    lane8 = lax.broadcasted_iota(jnp.int32, (8, LANES), 1)
    tile = jnp.zeros((8, LANES), F32)
    for k in range(PER):
        tile = jnp.where(lane8 == (cols * PER + k) % LANES, ntv[k] + nsv[k], tile)
    gbuf[x] = jnp.where(row8 == me, tile, 0.0)

    def gain_copy(i):
        return copy_to(gbuf.at[i], gbuf.at[i], send.at[3], small_recv.at[0], (c, cols))

    loads[0].wait()
    met = jnp.where(y % 2 == 0, 2, 1) + jnp.where(z == 0, 0, 2)
    pl.semaphore_wait(barrier, 4 - c + jnp.where(head, met, 0))
    for i in range(1, NX):
        @pl.when(x == i)
        def _(i=i):
            gain_copy(i).start()
    both_ways(0)

    @pl.when(c == 0)
    def _():
        signal(here, partner)

    @pl.when(head & (y == 0))
    def _():
        for peer in (at_y(1), at_y(NY - 1)):
            signal(y_token.at[0], peer)

    @pl.when(head & (z != 0))
    def _():
        for peer in (at_z(1), at_z(NZ - 1)):
            signal(z_token.at[0], peer)

    def dot(a, b):
        return jnp.dot(a, b, preferred_element_type=F32)

    loads[3].wait()
    loads[5].wait()
    for k in range(2):
        ht[k] = (hv[k].astype(F32).T * 2.0).astype(BF16)
    part[WIDE + TAIL:512, :] = jnp.zeros((512 - WIDE - TAIL, LANES), F32)

    for k in range(2):
        loads[4 + 2 * k].wait()
        if k == 1:
            loads[7].wait()
        for q in range(WIDE // STEP):
            r = slice(STEP * q, STEP * q + STEP)
            if k == 0:
                w = raw[r, mine].astype(F32) + dot(ht[0, r, :], low[:, mine])
            else:
                w = tuv[r, :].astype(F32) + dot(ht[1, r, :], luv[...])
                lat[r, :] = w
            w = w * w
            s = w[:, 0:LANES]
            for t in range(1, STRIPS):
                s = s + w[:, LANES * t:LANES * t + LANES]
            if k == 0:
                part[r, :] = s
            elif r.stop <= MAIN:
                part[512 + r.start:512 + r.stop, :] = s
            else:
                part[512 + r.start:512 + MAIN, :] = s[:MAIN - r.start]
                part[WIDE:WIDE + TAIL, :] = s[MAIN - r.start:]

    sums[c * NX + x] = jnp.concatenate(
        [jnp.sum(part[LANES * t:LANES * t + LANES, :].T, axis=0, keepdims=True) for t in range(7)]
        + [jnp.zeros((1, LANES), F32)], axis=0)

    def sum_copy(peer, recv):
        return remote(sums.at[c * NX + x], send.at[4], small_recv.at[recv], peer)

    for peer in rail:
        sum_copy(peer, 1).start()
    for n in (*LOW, *RAW[1:]):
        both_ways(n)

    def tokens(step):
        for peer in (at_z(1 << step), at_z(NZ - (1 << step))):
            signal(z_token.at[step], peer)

    @pl.when(head & (z != 0))
    def _():
        pl.semaphore_wait(z_token.at[0], 2)
        tokens(1)
        pl.semaphore_wait(z_token.at[1], 2)
        tokens(2)

    def first_tokens():
        pl.semaphore_wait(z_token.at[0], 2)
        tokens(0)
        tokens(1)

    @pl.when(head & (cols == 0))
    def _():
        first_tokens()

    eager = (cols == 0) & (c == 1)

    @pl.when(eager)
    def _():
        for n in (0, *LOW, *RAW[1:]):
            pass_on(n, False)

    @pl.when(c == 1)
    def _():
        pl.semaphore_wait(here, 1)

    def gains_in():
        return remote(gbuf.at[pl.ds(0, 3)], send.at[3], small_recv.at[0], partner)

    def rail_gains():
        return (gbuf[0] + gbuf[1]) + (gbuf[2] + gbuf[3])

    def gains_over():
        return copy_to(gbuf.at[5], gbuf.at[4], send.at[3], small_recv.at[2], partner)

    @pl.when(me == 1)
    def _():
        gains_in().wait_recv()
        gbuf[5] = rail_gains()
        gains_over().start()

    remote(sums.at[pl.ds(0, 3)], send.at[4], small_recv.at[1], partner).wait_recv()
    rail_sums = remote(sums.at[pl.ds(c * NX, NX)], send.at[5], small_recv.at[3], partner)
    rail_sums.start()
    own_raw = remote(raw.at[:, mine], send.at[0], d_recv.at[0], partner)
    own_low = remote(low.at[:, mine], send.at[1], d_recv.at[1], partner)
    own_raw.start()
    own_low.start()
    remote(sums.at[pl.ds((1 - c) * NX, NX)], send.at[5], small_recv.at[3], partner).wait_recv()

    total = sums[0]
    for s in range(1, GROUP):
        total = total + sums[s % NC * NX + s // NC]
    column = jnp.sqrt(total)
    inverse = jnp.concatenate([1.0 / column, jnp.zeros((LANES - 8, LANES), F32)], axis=0).T

    def spread_out(k):
        for t in range(3):
            spread[k, LANES * t:LANES * t + LANES, :] = jnp.broadcast_to(
                inverse[:, 4 * k + t:4 * k + t + 1], (LANES, LANES))
        spread[k, MAIN:, :] = jnp.broadcast_to(
            inverse[TAIL * k:TAIL * k + TAIL, 3:4], (TAIL, LANES))

    spread_out(1)
    for n in UP:
        t = n - STRIPS - 2
        out_u[:, lanes(me, t * LANES, LANES)] = (lat[:, t * LANES:t * LANES + LANES] * spread[1]).astype(BF16)
        both_ways(n)
        across(OWN, n).start()
    spread_out(0)

    col_g[...] = jnp.concatenate(
        [column[0:1], column[1:2], column[2:3], column[3:4]], axis=1)[:, :WIDE]
    col_u[...] = jnp.concatenate(
        [column[4:5], column[5:6], column[6:7], pltpu.roll(column, LANES - TAIL, axis=1)[3:4]], axis=1)[:, :WIDE]

    y_copies = [copy_to(ybuf.at[0], ybuf.at[i + 1], send.at[6], small_recv.at[4], at_y(dy))
                for i, dy in enumerate((1, NY - 1, 2))]

    def y_all():
        return remote(ybuf.at[pl.ds(0, 3)], send.at[6], small_recv.at[4], partner)

    def z_copy(d):
        return copy_to(zbuf.at[0], zbuf.at[d], send.at[7], small_recv.at[5], at_z(d))

    def z_all():
        return remote(zbuf.at[pl.ds(0, NZ - 1)], send.at[7], small_recv.at[5], partner)

    @pl.when(head & (y % 2 == 1))
    def _():
        pl.semaphore_wait(y_token.at[0], 1)
        for peer in (at_y(1), at_y(NY - 1)):
            signal(y_token.at[1], peer)

    @pl.when(head & (y % 2 == 0))
    def _():
        pl.semaphore_wait(y_token.at[1], 2)

    @pl.when(head)
    def _():
        gains_in().wait_recv()
        gains_over().wait_recv()
        ybuf[0] = rail_gains() + gbuf[4]
        for copy in y_copies:
            copy.start()

    @pl.when(head & (z == 0) & (y != 0))
    def _():
        first_tokens()

    def pass_group(group):
        @pl.when(jnp.logical_not(eager))
        def _():
            for n in group:
                pass_on(n)

    pass_group((0, *LOW, *RAW[1:3]))

    @pl.when(head & (z == 0))
    def _():
        pl.semaphore_wait(z_token.at[1], 2)
        tokens(2)

    @pl.when(head)
    def _():
        y_all().wait_recv()
        zbuf[0] = (ybuf[0] + ybuf[1]) + (ybuf[2] + ybuf[3])

    def z_wave():
        pl.semaphore_wait(z_token.at[2], 2)
        for d in range(1, NZ):
            z_copy(d).start()

    @pl.when(head & (z != 0))
    def _():
        z_wave()

    pass_group(RAW[3:])

    @pl.when(eager)
    def _():
        for k in (LEFT, RIGHT):
            for n in (*RAW, *LOW):
                across(k, n).start()

    crossed(raw.at[:, pl.ds(0, 3 * ROWS)], 0).wait_recv()
    crossed(low.at[:, pl.ds(0, 3 * ROWS)], 1).wait_recv()

    def finish(shard):
        w = lanes(shard)
        for q in range(WIDE // STEP):
            r = slice(STEP * q, STEP * q + STEP)
            s = spread[0, r, :]
            v = raw[r, w].astype(F32) + dot(ht[0, r, :], low[:, w])
            out_g[r, w] = (v * jnp.concatenate([s] * STRIPS, axis=1)).astype(BF16)

    def finish_near(i, _):
        d = i // NC
        finish(chip(d + d // 2, i % NC))
        return 0

    lax.fori_loop(0, 3 * NC, finish_near, 0)

    @pl.when(head & (z == 0))
    def _():
        z_wave()

    for n in UP[:2]:
        pass_on(n)

    def norm_copy(i, dev):
        return remote(norm, n_send.at[i], small_recv.at[7 if i == 3 else 6], dev)

    @pl.when(head)
    def _():
        z_all().wait_recv()
        tiles = [jnp.zeros((8, LANES), F32) for _ in range(5)]
        for d in range(NZ):
            start = ((z + NZ - d) % NZ) * NY * PER
            for t in range(5):
                place = lane8 + LANES * t
                tiles[t] = jnp.where((place >= start) & (place < start + NY * PER), zbuf[d], tiles[t])
        for t in range(5):
            nscr[pl.ds(t, 8, stride=5), :] = tiles[t]
        norm[...] = nscr[...].astype(BF16)

    for n in UP[2:3]:
        pass_on(n)

    @pl.when(head)
    def _():
        for i, dev in enumerate((*rail, partner)):
            norm_copy(i, dev).start()

    for n in UP[3:]:
        pass_on(n)

    far_lanes = lanes(source[FAR])
    remote(raw.at[:, far_lanes], send.at[0], far_recv.at[0], plus).wait_recv()
    remote(raw.at[:, far_lanes], send.at[0], d_recv.at[2], partner).start()
    remote(low.at[:, far_lanes], send.at[1], far_recv.at[1], plus).wait_recv()
    remote(low.at[:, far_lanes], send.at[1], d_recv.at[3], partner).start()
    crossed(raw.at[:, far_lanes], 2).wait_recv()
    crossed(low.at[:, far_lanes], 3).wait_recv()

    def finish_far(i, _):
        finish(chip(2, i))
        return 0

    lax.fori_loop(0, NC, finish_far, 0)

    @pl.when((c == 0) & jnp.logical_not(head))
    def _():
        norm_copy(0, plus).wait_recv()
        norm_copy(3, partner).start()

    rail_sums.wait_send()
    remote(sums.at[pl.ds(0, 3)], send.at[4], small_recv.at[1], partner).wait_send()

    @pl.when((x > 0) | (me == 1))
    def _():
        gains_over().wait_send()

    @pl.when(head)
    def _():
        y_all().wait_send()
        z_all().wait_send()

    for n in UP[:-1]:
        onward(n, FAR).wait_recv()
        across(FAR, n).start()

    @pl.when(c == 1)
    def _():
        norm_copy(3, partner).wait_recv()

    @pl.when(c == 0)
    def _():
        norm_copy(3, partner).wait_send()

    @pl.when(head)
    def _():
        for i, dev in enumerate(rail):
            norm_copy(i, dev).wait_send()

    crossed(raw.at[:, pl.ds(0, 7 * ROWS)], 0).wait_send()
    remote(low.at[:, pl.ds(0, 7 * ROWS)], send.at[1], d_recv.at[1], partner).wait_send()

    for n in UP[-1:]:
        onward(n, FAR).wait_recv()
        across(FAR, n).start()
    remote(out_u.at[:, pl.ds(0, 7 * ROWS)], send.at[2], d_recv.at[4], partner).wait_send()
    crossed(out_u.at[:, pl.ds(0, 4 * ROWS)], 4).wait_recv()


def write_kernel(*refs):
    n = (len(refs) - 1) // 2
    sources, targets, sem = refs[:n], refs[n:2 * n], refs[2 * n]
    copies = []
    for src, dst in zip(sources, targets):
        tall = src.shape[0] == WIDE
        for q in range(WIDE // STEP if tall else 1):
            r = pl.ds(q * STEP, STEP) if tall else slice(None)
            copies.append(pltpu.make_async_copy(src.at[r, :], dst.at[r, :], sem.at[len(copies)]))
    for copy in copies:
        copy.start()
    for copy in copies:
        copy.wait()


def on_device(tg, lg, hg, tu, lu, hu, nt, ns):
    dma, regular = pltpu.SemaphoreType.DMA, pltpu.SemaphoreType.REGULAR
    hbm = pl.BlockSpec(memory_space=pltpu.HBM)
    vmem = pl.BlockSpec(memory_space=pltpu.VMEM)
    results = (
        ((WIDE, D_MODEL), BF16), ((WIDE, D_MODEL), BF16),
        ((1, WIDE), F32), ((1, WIDE), F32), ((NORM_ROWS, LANES), BF16),
    )
    made = pl.pallas_call(
        gather_kernel,
        name="gather_weights",
        out_shape=tuple(pltpu.VMEM(*r) for r in results),
        in_specs=[hbm] * 8,
        out_specs=(vmem,) * 5,
        scratch_shapes=[
            pltpu.VMEM((WIDE, D_MODEL), BF16), pltpu.VMEM((RANK, D_MODEL), BF16),
            pltpu.VMEM((WIDE, ROWS), BF16), pltpu.VMEM((RANK, ROWS), BF16),
            pltpu.VMEM((2, RANK, WIDE), BF16), pltpu.VMEM((2, WIDE, RANK), BF16),
            pltpu.SMEM((PER,), F32), pltpu.SMEM((PER,), F32),
            pltpu.VMEM((WIDE, ROWS), F32), pltpu.VMEM((7 * LANES, LANES), F32),
            pltpu.VMEM((2, WIDE, LANES), F32), pltpu.VMEM((GROUP, 8, LANES), F32),
            pltpu.VMEM((6, 8, LANES), F32), pltpu.VMEM((NY, 8, LANES), F32), pltpu.VMEM((NZ, 8, LANES), F32),
            pltpu.VMEM((NORM_ROWS, LANES), F32),
            dma((8,)), regular, regular((2,)), regular((3,)),
            dma((8,)), dma((PIECES,)), dma((PIECES,)), dma((2 + STRIPS,)), dma((5,)), dma((8,)), dma((4,)),
        ],
        compiler_params=pltpu.CompilerParams(
            collective_id=0, has_side_effects=True, vmem_limit_bytes=24 << 20),
    )(*(pltpu.with_memory_space_constraint(a, pltpu.HBM) for a in (tg.T, lg.T, hg, tu.T, lu.T, hu, nt, ns)))
    gate, up, col_g, col_u, norm = pl.pallas_call(
        write_kernel,
        name="write_results",
        out_shape=tuple(jax.ShapeDtypeStruct(*r) for r in results),
        in_specs=[vmem] * 5,
        out_specs=(hbm,) * 5,
        scratch_shapes=[dma((13,))],
        compiler_params=pltpu.CompilerParams(vmem_limit_bytes=4 << 20),
    )(*(pltpu.with_memory_space_constraint(a, pltpu.VMEM) for a in made))
    return gate.T, up.T, col_g.reshape(WIDE), col_u.reshape(WIDE), norm.reshape(D_MODEL)


def solution(mesh):
    return jax.shard_map(
        on_device,
        mesh=mesh,
        in_specs=(
            P("zero", "cols"), P("zero", None), P(None, "cols"),
            P("zero", "cols"), P("zero", None), P(None, "cols"),
            P(("zero", "cols")), P(("zero", "cols")),
        ),
        out_specs=(P(None, "cols"), P(None, "cols"), P("cols"), P("cols"), P()),
        check_vma=False,
    )
```

time: 54.7 us -> 49 us (0.90)
  Pallas kernels: 53.9 us -> 48.2 us
    pallas_call x1, Pallas kernels: 50.6 us -> 44.8 us  [on_device(): pl.pallas_call(gather_kernel, name='gather_weights', out_shape=tuple((plt...]
where the time goes in v3:
time: 49 us; the launch traced here: 48.8 us
  Pallas kernels  48.2 us (98%)
  between operations  0.64 us (1%)
    pallas_call x1, Pallas kernels, on_device(): pl.pallas_call(gather_kernel, name='gather_weights', out_shape=tuple((plt...  44.8 us
    pallas_call x1, Pallas kernels, on_device(): pl.pallas_call(write_kernel, name='write_results', out_shape=tuple((jax.S...  3.37 us

profile of v3, /device:TPU:1, one launch (start us, length us, event | category | flops | bytes accessed | tf_op | source)
XLA Modules:
  0.0 48.8 jit_solution(17823744391423058828)
XLA Ops:
  0.6 44.8 %gather_weights.1 = (bf16[400,5120]{1,0:T(8,128)(2,1)S(1)}, bf16[400,5120]{1,0:T(8,128)(2,1)S(1)}, f32[1,400]{1,0:T(1,128)S(1)}, f32[1,400]{1,0:T(1,128)S(1)}, bf16[40,128]{1,0:T(8,128)(2,1)S(1)}) custom-call(bf16[400,640]{1,0:T(8,128)(2,1)} %bitcast.9, bf16[64,640]{1,0:T(8,128)(2,1)} %bitcast.11, bf16[64,400]{1,0:T(8,128)(2,1)} %hg.1, ...), custom_call_target="tpu_custom_call" | custom-call | tf_op jit(solution)/shard_map/gather_weights/pallas_call | solution.py:517
  45.5 3.4 %write_results.1 = (bf16[400,5120]{1,0:T(8,128)(2,1)}, bf16[400,5120]{1,0:T(8,128)(2,1)}, f32[1,400]{1,0:T(1,128)}, f32[1,400]{1,0:T(1,128)}, bf16[40,128]{1,0:T(8,128)(2,1)}) custom-call(bf16[400,5120]{1,0:T(8,128)(2,1)S(1)} %get-tuple-element.15.refs_0_, bf16[400,5120]{1,0:T(8,128)(2,1)S(1)} %get-tuple-element.16.refs_1_, ...), custom_call_target="tpu_custom_call" | custom-call | tf_op jit(solution)/shard_map/write_results/pallas_call | solution.py:538

commit v4 on v3

--- a/solution.py
+++ b/solution.py
@@ -20,10 +20,10 @@
 NORM_ROWS = D_MODEL // LANES
 
 RAW = range(0, STRIPS)
-LOW = range(STRIPS, STRIPS + 2)
-UP = range(STRIPS + 2, 2 * STRIPS + 2)
-PIECES = 2 * STRIPS + 2
-BY_PLUS = (0, 2, 4, 5, 8, 10)
+UP = range(STRIPS, 2 * STRIPS)
+PIECES = 2 * STRIPS
+BY_PLUS = (0, 2, 4, 6, 8)
+QUARTER = RANK // NY
 OWN, LEFT, RIGHT, FAR = 0, 1, 2, 3
 
 
@@ -91,8 +91,9 @@
     for load in loads:
         load.start()
 
+    late = (z == 0) & (c == 0)
     for dy in (1, NY - 1):
-        @pl.when(head & (y != 0))
+        @pl.when((late & (y != 0)) | (jnp.logical_not(late) & ((y + dy) % NY != 0)))
         def _(dy=dy):
             signal(barrier, at_y(dy))
 
@@ -106,12 +107,10 @@
     def piece(shard, n):
         if n in RAW:
             return raw.at[:, lanes(shard, n * LANES, LANES)]
-        if n in LOW:
-            return low.at[pl.ds((n - STRIPS) * (RANK // 2), RANK // 2), lanes(shard)]
-        return out_u.at[:, lanes(shard, (n - STRIPS - 2) * LANES, LANES)]
+        return out_u.at[:, lanes(shard, (n - STRIPS) * LANES, LANES)]
 
     def sent(n):
-        return send.at[0 if n in RAW else 1 if n in LOW else 2]
+        return send.at[0 if n in RAW else 2]
 
     def by_plus(n, k=OWN):
         return remote(piece(source[k], n), sent(n), l_recv.at[n], plus)
@@ -121,10 +120,10 @@
 
     def onward(n, k=None):
         k, dev = (LEFT if k is None else k, plus) if n in BY_PLUS else (RIGHT if k is None else k, minus)
-        return remote(piece(source[k], n), sent(n), far_recv.at[0 if n in RAW else 1 if n in LOW else n - STRIPS], dev)
+        return remote(piece(source[k], n), sent(n), far_recv.at[0 if n in RAW else n - STRIPS + 1], dev)
 
     def across(k, n):
-        kind = (0 if n in RAW else 1) + (2 if k == FAR else 0) if n not in UP else 4
+        kind = 0 if n in RAW else 3
         return remote(piece(source[k], n), sent(n), d_recv.at[kind], partner)
 
     def crossed(ref, kind):
@@ -151,6 +150,32 @@
 
         for step in (from_left, from_right) if n in BY_PLUS else (from_right, from_left):
             step()
+
+    loads[0].wait()
+    met = 4 - c + jnp.where(late, jnp.where(y % 2 == 0, 2, 1), jnp.where(y == 0, 0, 2))
+    pl.semaphore_wait(barrier, met + jnp.where(head & (z != 0), 2, 0))
+    both_ways(0)
+
+    @pl.when(c == 0)
+    def _():
+        signal(here, partner)
+
+    def y_tokens(i):
+        for peer in (at_y(1), at_y(NY - 1)):
+            signal(y_token.at[i], peer)
+
+    @pl.when((late & (y == 0)) | (jnp.logical_not(late) & (y == 2)))
+    def _():
+        y_tokens(0)
+
+    @pl.when(jnp.logical_not(late) & (y % 2 == 1))
+    def _():
+        y_tokens(1)
+
+    @pl.when(head & (z != 0))
+    def _():
+        for peer in (at_z(1), at_z(NZ - 1)):
+            signal(z_token.at[0], peer)
 
     loads[1].wait()
     loads[2].wait()
@@ -164,28 +189,10 @@
     def gain_copy(i):
         return copy_to(gbuf.at[i], gbuf.at[i], send.at[3], small_recv.at[0], (c, cols))
 
-    loads[0].wait()
-    met = jnp.where(y % 2 == 0, 2, 1) + jnp.where(z == 0, 0, 2)
-    pl.semaphore_wait(barrier, 4 - c + jnp.where(head, met, 0))
     for i in range(1, NX):
         @pl.when(x == i)
         def _(i=i):
             gain_copy(i).start()
-    both_ways(0)
-
-    @pl.when(c == 0)
-    def _():
-        signal(here, partner)
-
-    @pl.when(head & (y == 0))
-    def _():
-        for peer in (at_y(1), at_y(NY - 1)):
-            signal(y_token.at[0], peer)
-
-    @pl.when(head & (z != 0))
-    def _():
-        for peer in (at_z(1), at_z(NZ - 1)):
-            signal(z_token.at[0], peer)
 
     def dot(a, b):
         return jnp.dot(a, b, preferred_element_type=F32)
@@ -228,7 +235,10 @@
 
     for peer in rail:
         sum_copy(peer, 1).start()
-    for n in (*LOW, *RAW[1:]):
+    quarter = pl.ds(pl.multiple_of(y * QUARTER, QUARTER), QUARTER)
+    for peer in rail:
+        remote(low.at[quarter, mine], send.at[1], small_recv.at[8], peer).start()
+    for n in RAW[1:]:
         both_ways(n)
 
     def tokens(step):
@@ -255,7 +265,7 @@
 
     @pl.when(eager)
     def _():
-        for n in (0, *LOW, *RAW[1:]):
+        for n in RAW[:3]:
             pass_on(n, False)
 
     @pl.when(c == 1)
@@ -280,10 +290,8 @@
     remote(sums.at[pl.ds(0, 3)], send.at[4], small_recv.at[1], partner).wait_recv()
     rail_sums = remote(sums.at[pl.ds(c * NX, NX)], send.at[5], small_recv.at[3], partner)
     rail_sums.start()
-    own_raw = remote(raw.at[:, mine], send.at[0], d_recv.at[0], partner)
-    own_low = remote(low.at[:, mine], send.at[1], d_recv.at[1], partner)
-    own_raw.start()
-    own_low.start()
+    remote(raw.at[:, mine], send.at[0], d_recv.at[0], partner).start()
+    remote(low.at[:, mine], send.at[1], d_recv.at[1], partner).start()
     remote(sums.at[pl.ds((1 - c) * NX, NX)], send.at[5], small_recv.at[3], partner).wait_recv()
 
     total = sums[0]
@@ -301,7 +309,7 @@
 
     spread_out(1)
     for n in UP:
-        t = n - STRIPS - 2
+        t = n - STRIPS
         out_u[:, lanes(me, t * LANES, LANES)] = (lat[:, t * LANES:t * LANES + LANES] * spread[1]).astype(BF16)
         both_ways(n)
         across(OWN, n).start()
@@ -324,15 +332,25 @@
     def z_all():
         return remote(zbuf.at[pl.ds(0, NZ - 1)], send.at[7], small_recv.at[5], partner)
 
-    @pl.when(head & (y % 2 == 1))
+    @pl.when(y % 2 == 1)
     def _():
         pl.semaphore_wait(y_token.at[0], 1)
-        for peer in (at_y(1), at_y(NY - 1)):
-            signal(y_token.at[1], peer)
-
-    @pl.when(head & (y % 2 == 0))
+
+    @pl.when(late & (y % 2 == 1))
+    def _():
+        y_tokens(1)
+
+    @pl.when(y % 2 == 0)
     def _():
         pl.semaphore_wait(y_token.at[1], 2)
+
+    def quarters(n, recv):
+        return remote(low.at[pl.ds(0, n * QUARTER), pl.ds(0, 3 * ROWS)], send.at[1], small_recv.at[recv], partner)
+
+    quarters(1, 8).wait_recv()
+    for shard in source[1:]:
+        for dy in (1, NY - 1, 2):
+            remote(low.at[quarter, lanes(shard)], send.at[1], small_recv.at[9], at_y(dy)).start()
 
     @pl.when(head)
     def _():
@@ -346,13 +364,10 @@
     def _():
         first_tokens()
 
-    def pass_group(group):
-        @pl.when(jnp.logical_not(eager))
-        def _():
-            for n in group:
-                pass_on(n)
-
-    pass_group((0, *LOW, *RAW[1:3]))
+    @pl.when(jnp.logical_not(eager))
+    def _():
+        for n in RAW[:3]:
+            pass_on(n)
 
     @pl.when(head & (z == 0))
     def _():
@@ -373,16 +388,20 @@
     def _():
         z_wave()
 
-    pass_group(RAW[3:])
-
     @pl.when(eager)
     def _():
         for k in (LEFT, RIGHT):
-            for n in (*RAW, *LOW):
+            for n in RAW[:3]:
                 across(k, n).start()
 
+    for n in RAW[3:]:
+        pass_on(n)
+
+    quarters(NY - 1, 9).wait_recv()
+    for shard in source[1:]:
+        remote(low.at[:, lanes(shard)], send.at[1], d_recv.at[1], partner).start()
     crossed(raw.at[:, pl.ds(0, 3 * ROWS)], 0).wait_recv()
-    crossed(low.at[:, pl.ds(0, 3 * ROWS)], 1).wait_recv()
+    crossed(low.at[:, pl.ds(0, 4 * ROWS)], 1).wait_recv()
 
     def finish(shard):
         w = lanes(shard)
@@ -436,10 +455,7 @@
     far_lanes = lanes(source[FAR])
     remote(raw.at[:, far_lanes], send.at[0], far_recv.at[0], plus).wait_recv()
     remote(raw.at[:, far_lanes], send.at[0], d_recv.at[2], partner).start()
-    remote(low.at[:, far_lanes], send.at[1], far_recv.at[1], plus).wait_recv()
-    remote(low.at[:, far_lanes], send.at[1], d_recv.at[3], partner).start()
     crossed(raw.at[:, far_lanes], 2).wait_recv()
-    crossed(low.at[:, far_lanes], 3).wait_recv()
 
     def finish_far(i, _):
         finish(chip(2, i))
@@ -487,8 +503,8 @@
     for n in UP[-1:]:
         onward(n, FAR).wait_recv()
         across(FAR, n).start()
-    remote(out_u.at[:, pl.ds(0, 7 * ROWS)], send.at[2], d_recv.at[4], partner).wait_send()
-    crossed(out_u.at[:, pl.ds(0, 4 * ROWS)], 4).wait_recv()
+    remote(out_u.at[:, pl.ds(0, 7 * ROWS)], send.at[2], d_recv.at[3], partner).wait_send()
+    crossed(out_u.at[:, pl.ds(0, 4 * ROWS)], 3).wait_recv()
 
 
 def write_kernel(*refs):
@@ -530,7 +546,7 @@
             pltpu.VMEM((6, 8, LANES), F32), pltpu.VMEM((NY, 8, LANES), F32), pltpu.VMEM((NZ, 8, LANES), F32),
             pltpu.VMEM((NORM_ROWS, LANES), F32),
             dma((8,)), regular, regular((2,)), regular((3,)),
-            dma((8,)), dma((PIECES,)), dma((PIECES,)), dma((2 + STRIPS,)), dma((5,)), dma((8,)), dma((4,)),
+            dma((8,)), dma((PIECES,)), dma((PIECES,)), dma((1 + STRIPS,)), dma((4,)), dma((10,)), dma((4,)),
         ],
         compiler_params=pltpu.CompilerParams(
             collective_id=0, has_side_effects=True, vmem_limit_bytes=24 << 20),

time: 49 us -> 47.1 us (0.961)
  Pallas kernels: 48.2 us -> 46.3 us
    pallas_call x1, Pallas kernels: 44.8 us -> 42.9 us  [on_device(): pl.pallas_call(gather_kernel, name='gather_weights', out_shape=tuple((plt...]
where the time goes in v4:
time: 47.1 us; the launch traced here: 46.9 us
  Pallas kernels  46.3 us (98%)
  between operations  0.64 us (1%)
    pallas_call x1, Pallas kernels, on_device(): pl.pallas_call(gather_kernel, name='gather_weights', out_shape=tuple((plt...  42.9 us
    pallas_call x1, Pallas kernels, on_device(): pl.pallas_call(write_kernel, name='write_results', out_shape=tuple((jax.S...  3.37 us

profile of v4, /device:TPU:1, one launch (start us, length us, event | category | flops | bytes accessed | tf_op | source)
XLA Modules:
  0.0 46.9 jit_solution(10500034718706048710)
XLA Ops:
  0.6 42.9 %gather_weights.1 = (bf16[400,5120]{1,0:T(8,128)(2,1)S(1)}, bf16[400,5120]{1,0:T(8,128)(2,1)S(1)}, f32[1,400]{1,0:T(1,128)S(1)}, f32[1,400]{1,0:T(1,128)S(1)}, bf16[40,128]{1,0:T(8,128)(2,1)S(1)}) custom-call(bf16[400,640]{1,0:T(8,128)(2,1)} %bitcast.9, bf16[64,640]{1,0:T(8,128)(2,1)} %bitcast.11, bf16[64,400]{1,0:T(8,128)(2,1)} %hg.1, ...), custom_call_target="tpu_custom_call" | custom-call | tf_op jit(solution)/shard_map/gather_weights/pallas_call | solution.py:533
  43.6 3.4 %write_results.1 = (bf16[400,5120]{1,0:T(8,128)(2,1)}, bf16[400,5120]{1,0:T(8,128)(2,1)}, f32[1,400]{1,0:T(1,128)}, f32[1,400]{1,0:T(1,128)}, bf16[40,128]{1,0:T(8,128)(2,1)}) custom-call(bf16[400,5120]{1,0:T(8,128)(2,1)S(1)} %get-tuple-element.15.refs_0_, bf16[400,5120]{1,0:T(8,128)(2,1)S(1)} %get-tuple-element.16.refs_1_, ...), custom_call_target="tpu_custom_call" | custom-call | tf_op jit(solution)/shard_map/write_results/pallas_call | solution.py:554

commit v5 on v4

--- a/solution.py
+++ b/solution.py
@@ -31,7 +31,7 @@
     tg, lg, hg, tu, lu, hu, nt, ns,
     out_g, out_u, col_g, col_u, norm,
     raw, low, tuv, luv, hv, ht, ntv, nsv,
-    lat, part, spread, sums, gbuf, ybuf, zbuf, nscr,
+    lat, part, spread, sums, ybuf, zbuf, nscr,
     load_sem, here, y_token, z_token,
     send, l_recv, r_recv, far_recv, d_recv, small_recv, n_send,
 ):
@@ -72,7 +72,10 @@
 
     mine = lanes(me)
 
-    head = me == 0
+    head = c == 0
+    first = pltpu.make_async_copy(
+        tg.at[:, pl.ds(0, LANES)], raw.at[:, lanes(me, 0, LANES)], load_sem.at[8])
+    first.start()
     barrier = pltpu.get_barrier_semaphore()
     for peer in rail:
         signal(barrier, peer)
@@ -84,14 +87,14 @@
     loads = [
         pltpu.make_async_copy(a, b, load_sem.at[i])
         for i, (a, b) in enumerate(
-            ((tg, raw.at[:, mine]), (nt, ntv), (ns, nsv), (hg, hv.at[0]), (lg, low.at[:, mine]),
+            ((tg.at[:, pl.ds(LANES, ROWS - LANES)], raw.at[:, lanes(me, LANES, ROWS - LANES)]), (nt, ntv), (ns, nsv), (hg, hv.at[0]), (lg, low.at[:, mine]),
              (hu, hv.at[1]), (lu, luv), (tu, tuv))
         )
     ]
     for load in loads:
         load.start()
 
-    late = (z == 0) & (c == 0)
+    late = (z == 0) & head
     for dy in (1, NY - 1):
         @pl.when((late & (y != 0)) | (jnp.logical_not(late) & ((y + dy) % NY != 0)))
         def _(dy=dy):
@@ -151,7 +154,7 @@
         for step in (from_left, from_right) if n in BY_PLUS else (from_right, from_left):
             step()
 
-    loads[0].wait()
+    first.wait()
     met = 4 - c + jnp.where(late, jnp.where(y % 2 == 0, 2, 1), jnp.where(y == 0, 0, 2))
     pl.semaphore_wait(barrier, met + jnp.where(head & (z != 0), 2, 0))
     both_ways(0)
@@ -177,26 +180,10 @@
         for peer in (at_z(1), at_z(NZ - 1)):
             signal(z_token.at[0], peer)
 
-    loads[1].wait()
-    loads[2].wait()
-    row8 = lax.broadcasted_iota(jnp.int32, (8, LANES), 0)
-    lane8 = lax.broadcasted_iota(jnp.int32, (8, LANES), 1)
-    tile = jnp.zeros((8, LANES), F32)
-    for k in range(PER):
-        tile = jnp.where(lane8 == (cols * PER + k) % LANES, ntv[k] + nsv[k], tile)
-    gbuf[x] = jnp.where(row8 == me, tile, 0.0)
-
-    def gain_copy(i):
-        return copy_to(gbuf.at[i], gbuf.at[i], send.at[3], small_recv.at[0], (c, cols))
-
-    for i in range(1, NX):
-        @pl.when(x == i)
-        def _(i=i):
-            gain_copy(i).start()
-
     def dot(a, b):
         return jnp.dot(a, b, preferred_element_type=F32)
 
+    loads[0].wait()
     loads[3].wait()
     loads[5].wait()
     for k in range(2):
@@ -226,9 +213,16 @@
                 part[512 + r.start:512 + MAIN, :] = s[:MAIN - r.start]
                 part[WIDE:WIDE + TAIL, :] = s[MAIN - r.start:]
 
+    loads[1].wait()
+    loads[2].wait()
+    lane = lax.broadcasted_iota(jnp.int32, (1, LANES), 1)
+    own_gains = jnp.zeros((1, LANES), F32)
+    for k in range(PER):
+        own_gains = jnp.where(lane == (cols * PER + k) % LANES, ntv[k] + nsv[k], own_gains)
+
     sums[c * NX + x] = jnp.concatenate(
         [jnp.sum(part[LANES * t:LANES * t + LANES, :].T, axis=0, keepdims=True) for t in range(7)]
-        + [jnp.zeros((1, LANES), F32)], axis=0)
+        + [own_gains], axis=0)
 
     def sum_copy(peer, recv):
         return remote(sums.at[c * NX + x], send.at[4], small_recv.at[recv], peer)
@@ -236,7 +230,7 @@
     for peer in rail:
         sum_copy(peer, 1).start()
     quarter = pl.ds(pl.multiple_of(y * QUARTER, QUARTER), QUARTER)
-    for peer in rail:
+    for peer in (plus, minus):
         remote(low.at[quarter, mine], send.at[1], small_recv.at[8], peer).start()
     for n in RAW[1:]:
         both_ways(n)
@@ -245,51 +239,30 @@
         for peer in (at_z(1 << step), at_z(NZ - (1 << step))):
             signal(z_token.at[step], peer)
 
-    @pl.when(head & (z != 0))
-    def _():
-        pl.semaphore_wait(z_token.at[0], 2)
-        tokens(1)
-        pl.semaphore_wait(z_token.at[1], 2)
-        tokens(2)
-
-    def first_tokens():
-        pl.semaphore_wait(z_token.at[0], 2)
-        tokens(0)
-        tokens(1)
-
-    @pl.when(head & (cols == 0))
-    def _():
-        first_tokens()
-
     eager = (cols == 0) & (c == 1)
 
     @pl.when(eager)
     def _():
-        for n in RAW[:3]:
+        for n in RAW[:4]:
             pass_on(n, False)
 
     @pl.when(c == 1)
     def _():
         pl.semaphore_wait(here, 1)
-
-    def gains_in():
-        return remote(gbuf.at[pl.ds(0, 3)], send.at[3], small_recv.at[0], partner)
-
-    def rail_gains():
-        return (gbuf[0] + gbuf[1]) + (gbuf[2] + gbuf[3])
-
-    def gains_over():
-        return copy_to(gbuf.at[5], gbuf.at[4], send.at[3], small_recv.at[2], partner)
-
-    @pl.when(me == 1)
-    def _():
-        gains_in().wait_recv()
-        gbuf[5] = rail_gains()
-        gains_over().start()
 
     remote(sums.at[pl.ds(0, 3)], send.at[4], small_recv.at[1], partner).wait_recv()
     rail_sums = remote(sums.at[pl.ds(c * NX, NX)], send.at[5], small_recv.at[3], partner)
     rail_sums.start()
+
+    def low_block(rows, wide, recv):
+        return remote(low.at[pl.ds(0, rows), pl.ds(0, wide * ROWS)], send.at[1], small_recv.at[recv], partner)
+
+    low_block(QUARTER, 2, 8).wait_recv()
+    for core, k, dev in ((0, LEFT, plus), (1, RIGHT, minus)):
+        @pl.when(c == core)
+        def _(k=k, dev=dev):
+            remote(low.at[quarter, lanes(source[k])], send.at[1], small_recv.at[0], dev).start()
+
     remote(raw.at[:, mine], send.at[0], d_recv.at[0], partner).start()
     remote(low.at[:, mine], send.at[1], d_recv.at[1], partner).start()
     remote(sums.at[pl.ds((1 - c) * NX, NX)], send.at[5], small_recv.at[3], partner).wait_recv()
@@ -344,32 +317,39 @@
     def _():
         pl.semaphore_wait(y_token.at[1], 2)
 
-    def quarters(n, recv):
-        return remote(low.at[pl.ds(0, n * QUARTER), pl.ds(0, 3 * ROWS)], send.at[1], small_recv.at[recv], partner)
-
-    quarters(1, 8).wait_recv()
-    for shard in source[1:]:
+    def share(k, recv):
         for dy in (1, NY - 1, 2):
-            remote(low.at[quarter, lanes(shard)], send.at[1], small_recv.at[9], at_y(dy)).start()
+            remote(low.at[quarter, lanes(source[k])], send.at[1], small_recv.at[recv], at_y(dy)).start()
+
+    share(LEFT, 9)
+    share(RIGHT, 9)
 
     @pl.when(head)
     def _():
-        gains_in().wait_recv()
-        gains_over().wait_recv()
-        ybuf[0] = rail_gains() + gbuf[4]
+        ybuf[0] = jnp.concatenate(
+            [sums[s % NC * NX + s // NC][7:8, :] for s in range(GROUP)], axis=0)
         for copy in y_copies:
             copy.start()
 
-    @pl.when(head & (z == 0) & (y != 0))
-    def _():
-        first_tokens()
+    @pl.when(head & (z != 0))
+    def _():
+        pl.semaphore_wait(z_token.at[0], 2)
+        tokens(1)
+        pl.semaphore_wait(z_token.at[1], 2)
+        tokens(2)
+
+    @pl.when(late)
+    def _():
+        pl.semaphore_wait(z_token.at[0], 2)
+        tokens(0)
+        tokens(1)
 
     @pl.when(jnp.logical_not(eager))
     def _():
         for n in RAW[:3]:
             pass_on(n)
 
-    @pl.when(head & (z == 0))
+    @pl.when(late)
     def _():
         pl.semaphore_wait(z_token.at[1], 2)
         tokens(2)
@@ -391,17 +371,22 @@
     @pl.when(eager)
     def _():
         for k in (LEFT, RIGHT):
-            for n in RAW[:3]:
+            for n in RAW[:4]:
                 across(k, n).start()
 
-    for n in RAW[3:]:
-        pass_on(n)
-
-    quarters(NY - 1, 9).wait_recv()
-    for shard in source[1:]:
-        remote(low.at[:, lanes(shard)], send.at[1], d_recv.at[1], partner).start()
+    @pl.when(jnp.logical_not(eager))
+    def _():
+        pass_on(RAW[3])
+
+    pass_on(RAW[4])
+
+    low_block(2 * QUARTER, 3, 9).wait_recv()
+    for k in (LEFT, RIGHT):
+        remote(low.at[:, lanes(source[k])], send.at[1], d_recv.at[1], partner).start()
+    low_block(QUARTER, 1, 0).wait_recv()
+    share(FAR, 2)
     crossed(raw.at[:, pl.ds(0, 3 * ROWS)], 0).wait_recv()
-    crossed(low.at[:, pl.ds(0, 4 * ROWS)], 1).wait_recv()
+    crossed(low.at[:, pl.ds(0, 3 * ROWS)], 1).wait_recv()
 
     def finish(shard):
         w = lanes(shard)
@@ -418,19 +403,19 @@
 
     lax.fori_loop(0, 3 * NC, finish_near, 0)
 
-    @pl.when(head & (z == 0))
+    @pl.when(late)
     def _():
         z_wave()
 
     for n in UP[:2]:
         pass_on(n)
 
-    def norm_copy(i, dev):
-        return remote(norm, n_send.at[i], small_recv.at[7 if i == 3 else 6], dev)
-
-    @pl.when(head)
-    def _():
+    def norm_copy():
+        return remote(norm, n_send.at[0], small_recv.at[6], partner)
+
+    def all_gains():
         z_all().wait_recv()
+        lane8 = lax.broadcasted_iota(jnp.int32, (8, LANES), 1)
         tiles = [jnp.zeros((8, LANES), F32) for _ in range(5)]
         for d in range(NZ):
             start = ((z + NZ - d) % NZ) * NY * PER
@@ -441,20 +426,23 @@
             nscr[pl.ds(t, 8, stride=5), :] = tiles[t]
         norm[...] = nscr[...].astype(BF16)
 
-    for n in UP[2:3]:
+    @pl.when(head & (z != 0))
+    def _():
+        all_gains()
+
+    for n in UP[2:]:
         pass_on(n)
 
-    @pl.when(head)
-    def _():
-        for i, dev in enumerate((*rail, partner)):
-            norm_copy(i, dev).start()
-
-    for n in UP[3:]:
-        pass_on(n)
+    @pl.when(late)
+    def _():
+        all_gains()
 
     far_lanes = lanes(source[FAR])
+    low_block(3 * QUARTER, 1, 2).wait_recv()
+    remote(low.at[:, far_lanes], send.at[1], d_recv.at[4], partner).start()
     remote(raw.at[:, far_lanes], send.at[0], far_recv.at[0], plus).wait_recv()
     remote(raw.at[:, far_lanes], send.at[0], d_recv.at[2], partner).start()
+    crossed(low.at[:, far_lanes], 4).wait_recv()
     crossed(raw.at[:, far_lanes], 2).wait_recv()
 
     def finish_far(i, _):
@@ -463,17 +451,12 @@
 
     lax.fori_loop(0, NC, finish_far, 0)
 
-    @pl.when((c == 0) & jnp.logical_not(head))
-    def _():
-        norm_copy(0, plus).wait_recv()
-        norm_copy(3, partner).start()
+    @pl.when(head)
+    def _():
+        norm_copy().start()
 
     rail_sums.wait_send()
     remote(sums.at[pl.ds(0, 3)], send.at[4], small_recv.at[1], partner).wait_send()
-
-    @pl.when((x > 0) | (me == 1))
-    def _():
-        gains_over().wait_send()
 
     @pl.when(head)
     def _():
@@ -486,16 +469,11 @@
 
     @pl.when(c == 1)
     def _():
-        norm_copy(3, partner).wait_recv()
-
-    @pl.when(c == 0)
-    def _():
-        norm_copy(3, partner).wait_send()
+        norm_copy().wait_recv()
 
     @pl.when(head)
     def _():
-        for i, dev in enumerate(rail):
-            norm_copy(i, dev).wait_send()
+        norm_copy().wait_send()
 
     crossed(raw.at[:, pl.ds(0, 7 * ROWS)], 0).wait_send()
     remote(low.at[:, pl.ds(0, 7 * ROWS)], send.at[1], d_recv.at[1], partner).wait_send()
@@ -543,10 +521,10 @@
             pltpu.SMEM((PER,), F32), pltpu.SMEM((PER,), F32),
             pltpu.VMEM((WIDE, ROWS), F32), pltpu.VMEM((7 * LANES, LANES), F32),
             pltpu.VMEM((2, WIDE, LANES), F32), pltpu.VMEM((GROUP, 8, LANES), F32),
-            pltpu.VMEM((6, 8, LANES), F32), pltpu.VMEM((NY, 8, LANES), F32), pltpu.VMEM((NZ, 8, LANES), F32),
+            pltpu.VMEM((NY, 8, LANES), F32), pltpu.VMEM((NZ, 8, LANES), F32),
             pltpu.VMEM((NORM_ROWS, LANES), F32),
-            dma((8,)), regular, regular((2,)), regular((3,)),
-            dma((8,)), dma((PIECES,)), dma((PIECES,)), dma((1 + STRIPS,)), dma((4,)), dma((10,)), dma((4,)),
+            dma((9,)), regular, regular((2,)), regular((3,)),
+            dma((8,)), dma((PIECES,)), dma((PIECES,)), dma((1 + STRIPS,)), dma((5,)), dma((10,)), dma((1,)),
         ],
         compiler_params=pltpu.CompilerParams(
             collective_id=0, has_side_effects=True, vmem_limit_bytes=24 << 20),

time: 47.1 us -> 46.7 us (level)
  no operation moved by 1% of the time
where the time goes in v5:
time: 46.7 us; the launch traced here: 46.5 us
  Pallas kernels  45.9 us (98%)
  between operations  0.64 us (1%)
    pallas_call x1, Pallas kernels, on_device(): pl.pallas_call(gather_kernel, name='gather_weights', out_shape=tuple((plt...  42.5 us
    pallas_call x1, Pallas kernels, on_device(): pl.pallas_call(write_kernel, name='write_results', out_shape=tuple((jax.S...  3.37 us

profile of v5, /device:TPU:1, one launch (start us, length us, event | category | flops | bytes accessed | tf_op | source)
XLA Modules:
  0.0 46.5 jit_solution(17421248081570026945)
XLA Ops:
  0.6 42.5 %gather_weights.1 = (bf16[400,5120]{1,0:T(8,128)(2,1)S(1)}, bf16[400,5120]{1,0:T(8,128)(2,1)S(1)}, f32[1,400]{1,0:T(1,128)S(1)}, f32[1,400]{1,0:T(1,128)S(1)}, bf16[40,128]{1,0:T(8,128)(2,1)S(1)}) custom-call(bf16[400,640]{1,0:T(8,128)(2,1)} %bitcast.9, bf16[64,640]{1,0:T(8,128)(2,1)} %bitcast.11, bf16[64,400]{1,0:T(8,128)(2,1)} %hg.1, ...), custom_call_target="tpu_custom_call" | custom-call | tf_op jit(solution)/shard_map/gather_weights/pallas_call | solution.py:511
  43.1 3.4 %write_results.1 = (bf16[400,5120]{1,0:T(8,128)(2,1)}, bf16[400,5120]{1,0:T(8,128)(2,1)}, f32[1,400]{1,0:T(1,128)}, f32[1,400]{1,0:T(1,128)}, bf16[40,128]{1,0:T(8,128)(2,1)}) custom-call(bf16[400,5120]{1,0:T(8,128)(2,1)S(1)} %get-tuple-element.15.refs_0_, bf16[400,5120]{1,0:T(8,128)(2,1)S(1)} %get-tuple-element.16.refs_1_, ...), custom_call_target="tpu_custom_call" | custom-call | tf_op jit(solution)/shard_map/write_results/pallas_call | solution.py:532

commit v6 on v5

--- a/solution.py
+++ b/solution.py
@@ -19,10 +19,10 @@
 PER = 10
 NORM_ROWS = D_MODEL // LANES
 
-RAW = range(0, STRIPS)
-UP = range(STRIPS, 2 * STRIPS)
-PIECES = 2 * STRIPS
-BY_PLUS = (0, 2, 4, 6, 8)
+RAW = range(0, 3)
+UP = range(3, 3 + STRIPS)
+PIECES = 3 + STRIPS
+BY_PLUS = (0, 1, 4, 6)
 QUARTER = RANK // NY
 OWN, LEFT, RIGHT, FAR = 0, 1, 2, 3
 
@@ -109,8 +109,8 @@
 
     def piece(shard, n):
         if n in RAW:
-            return raw.at[:, lanes(shard, n * LANES, LANES)]
-        return out_u.at[:, lanes(shard, (n - STRIPS) * LANES, LANES)]
+            return raw.at[:, lanes(shard, max(2 * n - 1, 0) * LANES, (2 if n else 1) * LANES)]
+        return out_u.at[:, lanes(shard, (n - UP[0]) * LANES, LANES)]
 
     def sent(n):
         return send.at[0 if n in RAW else 2]
@@ -123,7 +123,7 @@
 
     def onward(n, k=None):
         k, dev = (LEFT if k is None else k, plus) if n in BY_PLUS else (RIGHT if k is None else k, minus)
-        return remote(piece(source[k], n), sent(n), far_recv.at[0 if n in RAW else n - STRIPS + 1], dev)
+        return remote(piece(source[k], n), sent(n), far_recv.at[0 if n in RAW else n - UP[0] + 1], dev)
 
     def across(k, n):
         kind = 0 if n in RAW else 3
@@ -243,7 +243,7 @@
 
     @pl.when(eager)
     def _():
-        for n in RAW[:4]:
+        for n in RAW[:2]:
             pass_on(n, False)
 
     @pl.when(c == 1)
@@ -282,7 +282,7 @@
 
     spread_out(1)
     for n in UP:
-        t = n - STRIPS
+        t = n - UP[0]
         out_u[:, lanes(me, t * LANES, LANES)] = (lat[:, t * LANES:t * LANES + LANES] * spread[1]).astype(BF16)
         both_ways(n)
         across(OWN, n).start()
@@ -346,7 +346,7 @@
 
     @pl.when(jnp.logical_not(eager))
     def _():
-        for n in RAW[:3]:
+        for n in RAW[:2]:
             pass_on(n)
 
     @pl.when(late)
@@ -371,14 +371,10 @@
     @pl.when(eager)
     def _():
         for k in (LEFT, RIGHT):
-            for n in RAW[:4]:
+            for n in RAW[:2]:
                 across(k, n).start()
 
-    @pl.when(jnp.logical_not(eager))
-    def _():
-        pass_on(RAW[3])
-
-    pass_on(RAW[4])
+    pass_on(RAW[2])
 
     low_block(2 * QUARTER, 3, 9).wait_recv()
     for k in (LEFT, RIGHT):

time: 46.7 us -> 46.6 us (level)
  no operation moved by 1% of the time
where the time goes in v6:
time: 46.6 us; the launch traced here: 46.5 us
  Pallas kernels  45.8 us (98%)
  between operations  0.64 us (1%)
    pallas_call x1, Pallas kernels, on_device(): pl.pallas_call(gather_kernel, name='gather_weights', out_shape=tuple((plt...  42.5 us
    pallas_call x1, Pallas kernels, on_device(): pl.pallas_call(write_kernel, name='write_results', out_shape=tuple((jax.S...  3.37 us

profile of v6, /device:TPU:1, one launch (start us, length us, event | category | flops | bytes accessed | tf_op | source)
XLA Modules:
  0.0 46.5 jit_solution(489128678375568511)
XLA Ops:
  0.6 42.5 %gather_weights.1 = (bf16[400,5120]{1,0:T(8,128)(2,1)S(1)}, bf16[400,5120]{1,0:T(8,128)(2,1)S(1)}, f32[1,400]{1,0:T(1,128)S(1)}, f32[1,400]{1,0:T(1,128)S(1)}, bf16[40,128]{1,0:T(8,128)(2,1)S(1)}) custom-call(bf16[400,640]{1,0:T(8,128)(2,1)} %bitcast.9, bf16[64,640]{1,0:T(8,128)(2,1)} %bitcast.11, bf16[64,400]{1,0:T(8,128)(2,1)} %hg.1, ...), custom_call_target="tpu_custom_call" | custom-call | tf_op jit(solution)/shard_map/gather_weights/pallas_call | solution.py:507
  43.1 3.4 %write_results.1 = (bf16[400,5120]{1,0:T(8,128)(2,1)}, bf16[400,5120]{1,0:T(8,128)(2,1)}, f32[1,400]{1,0:T(1,128)}, f32[1,400]{1,0:T(1,128)}, bf16[40,128]{1,0:T(8,128)(2,1)}) custom-call(bf16[400,5120]{1,0:T(8,128)(2,1)S(1)} %get-tuple-element.15.refs_0_, bf16[400,5120]{1,0:T(8,128)(2,1)S(1)} %get-tuple-element.16.refs_1_, ...), custom_call_target="tpu_custom_call" | custom-call | tf_op jit(solution)/shard_map/write_results/pallas_call | solution.py:528
